TPU v7x, 8 devices: a whole 2x2x1 slice. The times are simulated.
8 devices in a mesh: dp: 2 (over z, y), tp: 4 (over x, core).
Axes of the slice: x: 2, y: 2, z: 1, core: 2. Of those that a mesh axis runs over, the one named last changes fastest.
Arguments:
- x: bfloat16 [64, 4096], P('dp'), parts along dimension 0
- k_cache: bfloat16 [64, 1024, 32, 128], P('dp', None, 'tp'), parts along dimension 0
- v_cache: bfloat16 [64, 1024, 32, 128], P('dp', None, 'tp'), parts along dimension 0
- seq_lens: int32 [64], P('dp'), parts along dimension 0
- nbr_enc: bfloat16 [64, 256, 896], P('dp', 'tp'), parts along dimension 0
- ln1_gain: float32 [4096], replicated
- ln1_bias: float32 [4096], replicated
- w_q: bfloat16 [4096, 4096], P(None, 'tp')
- w_k: bfloat16 [4096, 4096], P(None, 'tp')
- w_v: bfloat16 [4096, 4096], P(None, 'tp')
- w_o: bfloat16 [4096, 4096], P('tp')
- ln2_gain: float32 [4096], replicated
- ln2_bias: float32 [4096], replicated
- wq_c: bfloat16 [4096, 4096], P(None, 'tp')
- wk_c: bfloat16 [896, 4096], P(None, 'tp')
- wv_c: bfloat16 [896, 4096], P(None, 'tp')
- wo_c: bfloat16 [4096, 4096], P('tp')
- ln3_gain: float32 [4096], replicated
- ln3_bias: float32 [4096], replicated
- w_up: bfloat16 [4096, 16384], P(None, 'tp')
- w_down: bfloat16 [16384, 4096], P('tp')
Outputs:
- output 1: bfloat16 [64, 4096], P('dp'), parts along dimension 0
- output 2: bfloat16 [64, 32, 128], P('dp', 'tp'), parts along dimension 0
- output 3: bfloat16 [64, 32, 128], P('dp', 'tp'), parts along dimension 0
There are 2 independent parts. A program takes and returns all parts, laid end to end along the dimension named above; an argument that names none is the same for every part.
All inputs are finite; a program needn't handle non-finite values.
Results may differ from a plain program's by a relative error of at most 0.0149296.
Values are sent between devices in bfloat16 or wider.
A program may use at most 1 GiB of HBM per device.

v0:
```python
import jax
import jax.numpy as jnp
from jax import lax
from jax.sharding import PartitionSpec as P

LN_EPS = 1e-5


def layer_norm(values, ln_gain, ln_bias):
    row_mean = jnp.mean(values, axis=-1, keepdims=True)
    centred = values - row_mean
    row_var = jnp.mean(jnp.square(centred), axis=-1, keepdims=True)
    return (centred * lax.rsqrt(row_var + LN_EPS) * ln_gain + ln_bias).astype(jnp.bfloat16)


def project(operand, weight):
    return jnp.dot(operand, weight, preferred_element_type=jnp.float32).astype(jnp.bfloat16)


def self_attention(q_new, k_new, v_new, k_cache, v_cache, seq_lens, q_scale):
    ctx_len = k_cache.shape[1]
    s_old = jnp.einsum('bhd,bthd->bht', q_new, k_cache, preferred_element_type=jnp.float32) * q_scale
    valid = jnp.arange(ctx_len)[None, None, :] < seq_lens[:, None, None]
    s_old = jnp.where(valid, s_old, -1e30)
    s_new = jnp.einsum('bhd,bhd->bh', q_new, k_new, preferred_element_type=jnp.float32) * q_scale
    row_max = jnp.maximum(jnp.max(s_old, axis=-1), s_new)
    e_old = jnp.exp(s_old - row_max[..., None])
    e_new = jnp.exp(s_new - row_max)
    row_sum = jnp.sum(e_old, axis=-1) + e_new
    p_old = (e_old / row_sum[..., None]).astype(jnp.bfloat16)
    p_new = (e_new / row_sum).astype(jnp.bfloat16)
    head_out = jnp.einsum('bht,bthd->bhd', p_old, v_cache, preferred_element_type=jnp.float32) + p_new.astype(jnp.float32)[..., None] * v_new.astype(jnp.float32)
    return head_out.astype(jnp.bfloat16)


def cross_attention(q_cross, k_nbr, v_nbr, q_scale):
    scores = jnp.einsum('bhd,bnhd->bhn', q_cross, k_nbr, preferred_element_type=jnp.float32) * q_scale
    probs = jax.nn.softmax(scores, axis=-1).astype(jnp.bfloat16)
    return jnp.einsum('bhn,bnhd->bhd', probs, v_nbr, preferred_element_type=jnp.float32).astype(jnp.bfloat16)


def local_step(x, k_cache, v_cache, seq_lens, nbr_enc, ln1_gain, ln1_bias, w_q, w_k, w_v, w_o, ln2_gain, ln2_bias, wq_c, wk_c, wv_c, wo_c, ln3_gain, ln3_bias, w_up, w_down):
    batch = x.shape[0]
    heads = k_cache.shape[2]
    head_dim = k_cache.shape[3]
    q_scale = head_dim ** -0.5
    residual = x.astype(jnp.float32)
    a_norm = layer_norm(residual, ln1_gain, ln1_bias)
    q_new = project(a_norm, w_q).reshape(batch, heads, head_dim)
    k_new = project(a_norm, w_k).reshape(batch, heads, head_dim)
    v_new = project(a_norm, w_v).reshape(batch, heads, head_dim)
    self_out = self_attention(q_new, k_new, v_new, k_cache, v_cache, seq_lens, q_scale)
    self_part = project(self_out.reshape(batch, heads * head_dim), w_o)
    residual = residual + lax.psum(self_part, 'tp').astype(jnp.float32)
    c_norm = layer_norm(residual, ln2_gain, ln2_bias)
    q_cross = project(c_norm, wq_c).reshape(batch, heads, head_dim)
    enc_all = lax.all_gather(nbr_enc, 'tp', axis=1, tiled=True)
    nbr_tokens = enc_all.shape[1]
    k_nbr = jnp.einsum('bne,ef->bnf', enc_all, wk_c, preferred_element_type=jnp.float32).astype(jnp.bfloat16).reshape(batch, nbr_tokens, heads, head_dim)
    v_nbr = jnp.einsum('bne,ef->bnf', enc_all, wv_c, preferred_element_type=jnp.float32).astype(jnp.bfloat16).reshape(batch, nbr_tokens, heads, head_dim)
    cross_out = cross_attention(q_cross, k_nbr, v_nbr, q_scale)
    cross_part = project(cross_out.reshape(batch, heads * head_dim), wo_c)
    residual = residual + lax.psum(cross_part, 'tp').astype(jnp.float32)
    m_norm = layer_norm(residual, ln3_gain, ln3_bias)
    hidden = jax.nn.gelu(jnp.dot(m_norm, w_up, preferred_element_type=jnp.float32), approximate=False).astype(jnp.bfloat16)
    mlp_part = project(hidden, w_down)
    layer_out = (residual + lax.psum(mlp_part, 'tp').astype(jnp.float32)).astype(jnp.bfloat16)
    return layer_out, k_new, v_new


def solution(mesh):
    row_spec = P('dp', None)
    cache_spec = P('dp', None, 'tp', None)
    head_spec = P('dp', 'tp', None)
    vec_spec = P(None)
    col_split = P(None, 'tp')
    row_split = P('tp', None)
    in_specs = (row_spec, cache_spec, cache_spec, P('dp'), P('dp', 'tp', None), vec_spec, vec_spec, col_split, col_split, col_split, row_split, vec_spec, vec_spec, col_split, col_split, col_split, row_split, vec_spec, vec_spec, col_split, row_split)
    out_specs = (row_spec, head_spec, head_spec)
    return jax.shard_map(local_step, mesh=mesh, in_specs=in_specs, out_specs=out_specs, check_vma=False)
```

profile of v0, /device:TPU:0, one launch (start us, length us, event | category | flops | bytes accessed | tf_op | source)
XLA Modules:
  0.0 392.8 jit_solution(18159168705889056280)
XLA Ops:
  7.2 0.0 copy-start
  7.2 0.0 all-reduce.4.cloned.1.call-start
  7.2 1.2 convert_reduce_fusion
  8.5 1.2 fusion.24
  9.7 5.1 %convolution_convert_fusion.7 = bf16[32,1024]{1,0:T(8,128)(2,1)S(1)} fusion(bf16[4096,1024]{1,0:T(8,128)(2,1)} %param.28, bf16[32,4096]{1,0:T(8,128)(2,1)} %param.21, f32[4096]{0:T(1024)} %param.27, f32[4096]{0:T(1024)} %param.26, f32[32]{0:T(128)S(1)} %add_rsqrt_fusion.2, f32[32]{0:T(128)S(1)} %broadcast_multiply_fusion.2), kind=kOutput, calls=%fused_computation.24 | convolution fusion | flops 269254656 | bytes 8749312 | tf_op jit(solution)/shard_map/dot_general | solution.py:17
  14.8 0.1 reshape.119
  14.9 5.1 %fusion.16 = bf16[4,8,8,128]{3,1,2,0:T(8,128)(2,1)S(1)} fusion(bf16[4096,1024]{1,0:T(8,128)(2,1)} %param.29, bf16[32,4096]{1,0:T(8,128)(2,1)} %param.21, f32[4096]{0:T(1024)} %param.27, f32[4096]{0:T(1024)} %param.26, f32[32]{0:T(128)S(1)} %add_rsqrt_fusion.2, f32[32]{0:T(128)S(1)} %broadcast_multiply_fusion.2), kind=kOutput, calls=%fused_computation.25 | convolution fusion | flops 269254656 | bytes 8749312 | tf_op jit(solution)/shard_map/dot_general | solution.py:17
  20.0 0.0 copy-start.6
  20.1 0.1 iota_compare_fusion
  20.1 0.5 copy-done.6
  20.7 0.1 fusion.86
  20.8 0.0 copy-start.2
  20.8 0.0 copy-start.7
  20.8 26.1 %fusion.4 = f32[32,8,1,1024]{3,2,1,0:T(1,128)S(1)} fusion(bf16[32,8,128,1]{2,3,1,0:T(2,128)(2,1)S(1)} %reshape.119, bf16[32,1024,8,128]{3,2,1,0:T(8,128)(2,1)} %param.22), kind=kOutput, calls=%fused_computation.4 | convolution fusion | flops 67108864 | bytes 68222976 | tf_op jit(solution)/shard_map/bhd,bthd->bht/dot_general | solution.py:22
  47.0 0.4 fusion.21
  47.4 0.5 fusion.20
  47.9 0.4 fusion.37
  48.4 5.0 %fusion.17 = bf16[4,8,8,128]{3,1,2,0:T(8,128)(2,1)S(1)} fusion(bf16[4096,1024]{1,0:T(8,128)(2,1)} %param.30, bf16[32,4096]{1,0:T(8,128)(2,1)S(1)} %copy-done.2, f32[4096]{0:T(1024)S(1)} %copy-done.7, f32[4096]{0:T(1024)S(1)} %copy-done.8, f32[32]{0:T(128)S(1)} %add_rsqrt_fusion.2, f32[32]{0:T(128)S(1)} %broadcast_multiply_fusion.2), kind=kOutput, calls=%fused_computation.26 | convolution fusion | flops 269254656 | bytes 8749312 | tf_op jit(solution)/shard_map/dot_general | solution.py:17
  53.4 0.0 copy-start.5
  53.4 25.5 %fusion.2 = f32[32,8,1,128]{3,2,1,0:T(1,128)S(1)} fusion(bf16[32,1024,8,128]{3,2,1,0:T(8,128)(2,1)} %param.23, bf16[32,8,1024,1]{2,1,0,3:T(8,128)(2,1)S(1)} %fusion.37), kind=kOutput, calls=%fused_computation.2 | convolution fusion | flops 67108864 | bytes 67764224 | tf_op jit(solution)/shard_map/bht,bthd->bhd/dot_general | solution.py:32
  78.9 0.1 add_convert_fusion.9
  79.0 5.6 %convolution_convert_fusion.3 = bf16[32,4096]{1,0:T(8,128)(2,1)} fusion(bf16[1024,4096]{1,0:T(8,128)(2,1)} %param.31, bf16[4,8,8,128]{3,2,1,0:T(8,128)(2,1)S(1)} %bitcast.71), kind=kOutput, calls=%fused_computation.13 | convolution fusion | flops 268566528 | bytes 8716288 | tf_op jit(solution)/shard_map/dot_general | solution.py:17
  84.7 0.0 all-reduce.4.cloned.1.call-update
  84.7 0.0 all-gather.2.cloned.1.call-start
  84.7 0.7 all-gather.2.cloned.1.call-update
  85.4 0.2 all-reduce.6.cloned.1.call-start
  85.7 28.6 %all-reduce.4.cloned.1.call-done = bf16[32,4096]{1,0:T(8,128)(2,1)} async-done(((bf16[32,4096]{1,0:T(8,128)(2,1)}), bf16[32,4096]{1,0:T(8,128)(2,1)}) %all-reduce.4.cloned.1.call-update) | async-done | bytes 262160 | tf_op jit(solution)/shard_map/psum | solution.py:54
  114.3 1.1 fusion.39
  115.4 1.2 multiply_reduce_fusion.1
  116.6 5.1 %convolution_convert_fusion.4 = bf16[32,1024]{1,0:T(8,128)(2,1)S(1)} fusion(bf16[4096,1024]{1,0:T(8,128)(2,1)} %param.34, bf16[32,4096]{1,0:T(8,128)(2,1)} %all-reduce.4.cloned.1.call-done, bf16[32,4096]{1,0:T(8,128)(2,1)S(1)} %copy-done.2, f32[4096]{0:T(1024)S(1)} %copy-done.11, f32[4096]{0:T(1024)S(1)} %copy-done.12, f32[32]{0:T(128)S(1)} %add_rsqrt_fusion.1, ...), kind=kOutput, calls=%fused_computation.21 | convolution fusion | flops 269516800 | bytes 9011456 | tf_op jit(solution)/shard_map/dot_general | solution.py:17
  121.7 0.1 reshape.121
  121.8 86.2 %all-gather.2.cloned.1.call-done = bf16[32,256,896]{2,1,0:T(8,128)(2,1)} async-done(((bf16[32,64,896]{2,1,0:T(8,128)(2,1)}), bf16[32,256,896]{2,1,0:T(8,128)(2,1)}) %all-gather.2.cloned.1.call-update) | async-done | bytes 14680080 | tf_op jit(solution)/shard_map/all_gather | solution.py:57
  207.9 25.5 %convolution_convert_fusion = bf16[32,256,1024]{2,1,0:T(8,128)(2,1)} fusion(bf16[32,256,896]{2,1,0:T(8,128)(2,1)} %all-gather.2.cloned.1.call-done, bf16[896,1024]{1,0:T(8,128)(2,1)S(1)} %copy-done), kind=kOutput, calls=%fused_computation.10 | convolution fusion | flops 15040774144 | bytes 33292288 | tf_op jit(solution)/shard_map/bne,ef->bnf/dot_general | solution.py:59
  233.4 22.5 %copy.40 = bf16[32,256,1024]{1,2,0:T(8,128)(2,1)} copy(bf16[32,256,1024]{2,1,0:T(8,128)(2,1)} %convolution_convert_fusion) | data formatting | bytes 33554432 | tf_op jit(solution)/shard_map/reshape | solution.py:59
  255.9 8.0 %fusion.129 = f32[32,8,1,256]{3,2,1,0:T(1,128)S(1)} fusion(bf16[32,8,128,1]{2,3,1,0:T(2,128)(2,1)S(1)} %reshape.121, bf16[32,256,8,128]{1,3,2,0:T(8,128)(2,1)} %bitcast.69), kind=kOutput, calls=%fused_computation.164 | convolution fusion | flops 16777216 | bytes 17104896 | tf_op jit(solution)/shard_map/bhd,bnhd->bhn/dot_general | solution.py:37
  263.9 0.2 fusion.15
  264.1 24.9 %convert_bitcast_fusion = bf16[32,32,8,8,128]{4,3,2,1,0:T(8,128)(2,1)} fusion(bf16[32,256,896]{2,1,0:T(8,128)(2,1)} %all-gather.2.cloned.1.call-done, bf16[896,1024]{1,0:T(8,128)(2,1)} %param.36), kind=kOutput, calls=%fused_computation.9 | convolution fusion | flops 15040774144 | bytes 33292288 | tf_op jit(solution)/shard_map/bne,ef->bnf/dot_general | solution.py:60
  289.0 8.0 %fusion.6 = f32[32,8,1,128]{3,2,1,0:T(1,128)S(1)} fusion(bf16[32,32,8,8,128]{4,3,2,1,0:T(8,128)(2,1)} %convert_bitcast_fusion, bf16[32,8,256,1]{2,1,0,3:T(8,128)(2,1)S(1)} %fusion.15), kind=kOutput, calls=%fused_computation.6 | convolution fusion | flops 16777216 | bytes 17039360 | tf_op jit(solution)/shard_map/bhn,bnhd->bhd/dot_general | solution.py:39
  297.1 5.7 %convolution_convert_fusion.2 = bf16[32,4096]{1,0:T(8,128)(2,1)} fusion(bf16[1024,4096]{1,0:T(8,128)(2,1)} %param.37, bf16[4,8,8,128]{3,2,1,0:T(8,128)(2,1)S(1)} %bitcast.72), kind=kOutput, calls=%fused_computation.12 | convolution fusion | flops 268566528 | bytes 8716288 | tf_op jit(solution)/shard_map/dot_general | solution.py:17
  302.8 0.0 all-reduce.6.cloned.1.call-update
  302.8 0.3 all-reduce.8.cloned.1.call-start
  303.1 26.4 %all-reduce.6.cloned.1.call-done = bf16[32,4096]{1,0:T(8,128)(2,1)} async-done(((bf16[32,4096]{1,0:T(8,128)(2,1)}), bf16[32,4096]{1,0:T(8,128)(2,1)}) %all-reduce.6.cloned.1.call-update) | async-done | bytes 262160 | tf_op jit(solution)/shard_map/psum | solution.py:63
  329.5 1.2 fusion.125
  330.7 1.2 multiply_reduce_fusion
  331.9 25.5 %convolution_convert_fusion.1 = bf16[32,4096]{1,0:T(8,128)(2,1)} fusion(bf16[4096,4096]{1,0:T(8,128)(2,1)} %param.41, bf16[4096,4096]{1,0:T(8,128)(2,1)} %param.40, f32[4096]{0:T(1024)S(1)} %copy-done.9, f32[4096]{0:T(1024)S(1)} %copy-done.10, f32[32]{0:T(128)S(1)} %add_rsqrt_fusion, f32[32]{0:T(128)S(1)} %broadcast_multiply_fusion, ...), kind=kOutput, calls=%fused_computation.11 | convolution fusion | flops 2157445120 | bytes 68190464 | tf_op jit(solution)/shard_map/dot_general | solution.py:17
  357.5 0.0 all-reduce.8.cloned.1.call-update
  357.5 26.8 %all-reduce.8.cloned.1.call-done = bf16[32,4096]{1,0:T(8,128)(2,1)} async-done(((bf16[32,4096]{1,0:T(8,128)(2,1)}), bf16[32,4096]{1,0:T(8,128)(2,1)}) %all-reduce.8.cloned.1.call-update) | async-done | bytes 262160 | tf_op jit(solution)/shard_map/psum | solution.py:67
  384.2 1.8 add_convert_fusion
  (34 shorter events, 0.2 us)
Async XLA Ops:
  7.2 200.8 %copy-start = (bf16[896,1024]{1,0:T(8,128)(2,1)S(1)}, bf16[896,1024]{1,0:T(8,128)(2,1)}, u32[]{:S(2)}) copy-start(bf16[896,1024]{1,0:T(8,128)(2,1)} %param.35) | copy-start | bytes 5505028
  7.2 12.8 %copy-start.13 = (s32[32]{0:T(128)S(1)}, s32[32]{0:T(128)}, u32[]{:S(2)}) copy-start(s32[32]{0:T(128)} %param.24) | copy-start | bytes 388
  7.2 107.1 %all-reduce.4.cloned.1.call-start = ((), (), s32[]{:S(2)}) async-start(), calls=%async_computation | async-start | bytes 524288 | tf_op jit(solution)/shard_map/psum | solution.py:54
  20.0 0.6 copy-start.6
  20.8 27.5 %copy-start.2 = (bf16[32,4096]{1,0:T(8,128)(2,1)S(1)}, bf16[32,4096]{1,0:T(8,128)(2,1)}, u32[]{:S(2)}) copy-start(bf16[32,4096]{1,0:T(8,128)(2,1)} %param.21) | copy-start | bytes 786436
  20.8 27.5 %copy-start.7 = (f32[4096]{0:T(1024)S(1)}, f32[4096]{0:T(1024)}, u32[]{:S(2)}) copy-start(f32[4096]{0:T(1024)} %param.27) | copy-start | bytes 49156
  20.8 27.5 %copy-start.8 = (f32[4096]{0:T(1024)S(1)}, f32[4096]{0:T(1024)}, u32[]{:S(2)}) copy-start(f32[4096]{0:T(1024)} %param.26) | copy-start | bytes 49156
  53.4 25.5 %copy-start.5 = (bf16[4,8,8,128]{3,2,1,0:T(8,128)(2,1)}, bf16[4,8,8,128]{3,2,1,0:T(8,128)(2,1)S(1)}, u32[]{:S(2)}) copy-start(bf16[4,8,8,128]{3,2,1,0:T(8,128)(2,1)S(1)} %copy.44) | copy-start | bytes 196612
  78.9 37.7 %copy-start.11 = (f32[4096]{0:T(1024)S(1)}, f32[4096]{0:T(1024)}, u32[]{:S(2)}) copy-start(f32[4096]{0:T(1024)} %param.33) | copy-start | bytes 49156
  78.9 37.7 %copy-start.12 = (f32[4096]{0:T(1024)S(1)}, f32[4096]{0:T(1024)}, u32[]{:S(2)}) copy-start(f32[4096]{0:T(1024)} %param.32) | copy-start | bytes 49156
  84.7 123.2 %all-gather.2.cloned.1.call-start = ((), (), s32[]{:S(2)}) async-start(), calls=%async_computation.1 | async-start | bytes 18350080 | tf_op jit(solution)/shard_map/all_gather | solution.py:57
  85.4 244.1 %all-reduce.6.cloned.1.call-start = ((), (), s32[]{:S(2)}) async-start(), calls=%async_computation.2 | async-start | bytes 524288 | tf_op jit(solution)/shard_map/psum | solution.py:63
  297.0 32.5 %copy-start.3 = (bf16[32,4096]{1,0:T(8,128)(2,1)S(1)}, bf16[32,4096]{1,0:T(8,128)(2,1)}, u32[]{:S(2)}) copy-start(bf16[32,4096]{1,0:T(8,128)(2,1)} %all-reduce.4.cloned.1.call-done) | copy-start | bytes 786436
  297.0 34.9 %copy-start.9 = (f32[4096]{0:T(1024)S(1)}, f32[4096]{0:T(1024)}, u32[]{:S(2)}) copy-start(f32[4096]{0:T(1024)} %param.39) | copy-start | bytes 49156
  297.1 34.9 %copy-start.10 = (f32[4096]{0:T(1024)S(1)}, f32[4096]{0:T(1024)}, u32[]{:S(2)}) copy-start(f32[4096]{0:T(1024)} %param.38) | copy-start | bytes 49156
  302.8 81.5 %all-reduce.8.cloned.1.call-start = ((), (), s32[]{:S(2)}) async-start(), calls=%async_computation.3 | async-start | bytes 524288 | tf_op jit(solution)/shard_map/psum | solution.py:67
  331.9 52.3 %copy-start.4 = (bf16[32,4096]{1,0:T(8,128)(2,1)S(1)}, bf16[32,4096]{1,0:T(8,128)(2,1)}, u32[]{:S(2)}) copy-start(bf16[32,4096]{1,0:T(8,128)(2,1)} %all-reduce.6.cloned.1.call-done) | copy-start | bytes 786436
  331.9 54.1 %copy-start.1 = (bf16[896,1024]{1,0:T(8,128)(2,1)S(1)}, bf16[896,1024]{1,0:T(8,128)(2,1)}, u32[]{:S(2)}) copy-start(bf16[896,1024]{1,0:T(8,128)(2,1)} %param.35) | copy-start | bytes 5505028
Sparse Core Ops, SparseCore 0:
  84.8 29.4 all-reduce.3
  115.8 92.0 all-gather.1
  302.9 26.5 all-reduce.5
  357.6 26.5 all-reduce.7
where the time goes:
time: 397 us; the launch traced here: 393 us
  matrix products  175 us (44%)
  waiting for transfers between devices  169 us (43%)
  local copies, waits for them, and re-layouts  23.3 us (6%)
  between operations  14.3 us (4%)
  other arithmetic  10.8 us (3%)
    all_gather x1, waiting for transfers between devices, local_step(): enc_all = lax.all_gather(nbr_enc, 'tp', axis=1, tiled=True)  86.2 us
    dot_general x7, matrix products, project(): jnp.dot(operand, weight, preferred_element_type=jnp.float32)  57.1 us
    psum x1, waiting for transfers between devices, local_step(): residual = residual + lax.psum(self_part, 'tp').astype(jnp.float32)  28.6 us
    psum x1, waiting for transfers between devices, local_step(): lax.psum(mlp_part, 'tp').astype(jnp.float32)  26.8 us
    psum x1, waiting for transfers between devices, local_step(): residual = residual + lax.psum(cross_part, 'tp').astype(jnp.float32)  26.4 us
    dot_general x1, matrix products, self_attention(): jnp.einsum('bhd,bthd->bht', q_new, k_cache, preferred_element_type=jnp.fl...  26.1 us
    dot_general x1, matrix products, self_attention(): jnp.einsum('bht,bthd->bhd', p_old, v_cache, preferred_element_type=jnp.fl...  25.5 us
    dot_general x1, matrix products, local_step(): jnp.einsum('bne,ef->bnf', enc_all, wk_c, preferred_element_type=jnp.float32)  25.5 us
  transfers between devices with their start and end apart: 4, of which 4 were waited for; matrix products, arithmetic and copies ran while one was open for 2% of the time, Pallas kernels for 0%

commit v1 on v0

v1 whole, which is shorter than its diff:
```python
import jax
import jax.numpy as jnp
from jax import lax
from jax.experimental import pallas as pl
from jax.experimental.pallas import tpu as pltpu
from jax.sharding import PartitionSpec as P

LN_EPS = 1e-5
LOG2_E = 1.4426950408889634
W_SLOTS = 8
W_ROWS = 512
SPAN = 64
GROUP = 8
KV_SLOTS = 5


def attn_kernel(lens_ref, x_ref, g_ref, b_ref, wq_ref, wk_ref, wv_ref, kc_ref, vc_ref,
                o_ref, kn_ref, vn_ref,
                w_buf, k_buf, v_buf, a_scr, q_scr, qb_scr, k_scr, v_scr, s_scr, o_scr, acc_scr, item_row, item_src, item_pos, w_sem, k_sem, v_sem):
    batch, width = x_ref.shape
    heads = q_scr.shape[1]
    head_dim = q_scr.shape[2]
    rate = head_dim ** -0.5 * LOG2_E
    w_chunks = width // W_ROWS
    span_rows = SPAN * heads
    half = span_rows // 2
    weights = (wq_ref, wk_ref, wv_ref)

    def w_copy(index, src, row):
        slot = lax.rem(index, W_SLOTS)
        return pltpu.make_async_copy(src.at[pl.ds(row * W_ROWS, W_ROWS), :], w_buf.at[slot], w_sem.at[slot])

    for index in range(W_SLOTS):
        w_copy(jnp.int32(index), weights[index // w_chunks], index % w_chunks).start()

    def list_row(row, count):
        def list_span(span, count):
            item_row[count] = row
            item_src[count] = row
            item_pos[count] = span * span_rows
            return count + 1
        return lax.fori_loop(0, lax.div(lens_ref[row], SPAN), list_span, count)
    items = lax.fori_loop(0, batch, list_row, jnp.int32(0))
    groups = lax.div(items + (GROUP - 1), GROUP)
    for extra in range(GROUP):
        item_row[items + extra] = batch
        item_src[items + extra] = 0
        item_pos[items + extra] = 0

    def kv_start(group):
        slot = lax.rem(group, KV_SLOTS)
        for member in range(GROUP):
            item = group * GROUP + member
            rows = pl.ds(pl.multiple_of(item_pos[item], span_rows), span_rows)
            place = pl.ds(member * span_rows, span_rows)
            pltpu.make_async_copy(kc_ref.at[item_src[item], rows], k_buf.at[slot, place], k_sem.at[slot]).start()
            pltpu.make_async_copy(vc_ref.at[item_src[item], rows], v_buf.at[slot, place], v_sem.at[slot]).start()

    values = x_ref[...].astype(jnp.float32)
    row_mean = jnp.mean(values, axis=-1, keepdims=True)
    centred = values - row_mean
    row_var = jnp.mean(jnp.square(centred), axis=-1, keepdims=True)
    normed = (centred * lax.rsqrt(row_var + LN_EPS) * g_ref[...] + b_ref[...]).astype(jnp.bfloat16)
    for chunk in range(w_chunks):
        a_scr[chunk] = normed[:, chunk * W_ROWS:(chunk + 1) * W_ROWS]

    acc_scr[...] = jnp.zeros_like(acc_scr)

    def step(index, carry):
        which = lax.div(index, w_chunks)
        chunk = lax.rem(index, w_chunks)
        slot = lax.rem(index, W_SLOTS)
        w_copy(index, wq_ref, chunk).wait()
        acc_scr[which] += jnp.dot(a_scr[chunk], w_buf[slot], preferred_element_type=jnp.float32)
        later = index + W_SLOTS
        for source in range(1, 3):
            @pl.when(lax.div(later, w_chunks) == source)
            def _():
                w_copy(later, weights[source], lax.rem(later, w_chunks)).start()

        for ahead in range(KV_SLOTS - 1):
            @pl.when((index == 2 * w_chunks + ahead) & (ahead < groups))
            def _():
                kv_start(jnp.int32(ahead))
        return carry
    lax.fori_loop(0, 3 * w_chunks, step, 0)

    for which in range(3):
        out = acc_scr[which].astype(jnp.bfloat16)
        if which == 1:
            kn_ref[...] = out
        if which == 2:
            vn_ref[...] = out
        rounded = out.astype(jnp.float32)
        dest = (q_scr, k_scr, v_scr)[which]
        for head in range(heads):
            dest[0:batch, head, :] = rounded[:, head * head_dim:(head + 1) * head_dim]

    def prepare(row, carry):
        q = q_scr[row]
        zero = jnp.zeros_like(q)
        qb_scr[row] = jnp.concatenate([jnp.concatenate([q, zero], axis=1), jnp.concatenate([zero, q], axis=1)], axis=0).astype(jnp.bfloat16)
        s_scr[row] = jnp.broadcast_to(jnp.sum(q * k_scr[row], axis=-1, keepdims=True), q.shape)
        return carry
    lax.fori_loop(0, batch, prepare, 0, unroll=4)
    qb_scr[batch] = jnp.zeros(qb_scr.shape[1:], qb_scr.dtype)
    s_scr[batch] = jnp.zeros(s_scr.shape[1:], s_scr.dtype)
    v_scr[batch] = jnp.zeros(v_scr.shape[1:], v_scr.dtype)

    sub = lax.broadcasted_iota(jnp.int32, (2 * heads, half), 0)
    lane = lax.broadcasted_iota(jnp.int32, (2 * heads, half), 1)
    keep = ((lane ^ sub) & (heads - 1)) == 0

    def group_step(group, carry):
        run_max, run_sum, run_out = carry
        slot = lax.rem(group, KV_SLOTS)
        whole = pl.ds(0, GROUP * span_rows)

        @pl.when(group + KV_SLOTS - 1 < groups)
        def _():
            kv_start(group + KV_SLOTS - 1)
        pltpu.make_async_copy(kc_ref.at[0, whole], k_buf.at[slot], k_sem.at[slot]).wait()
        pltpu.make_async_copy(vc_ref.at[0, whole], v_buf.at[slot], v_sem.at[slot]).wait()
        rows = [item_row[group * GROUP + member] for member in range(GROUP)]
        scores = []
        for member in range(GROUP):
            base = member * span_rows
            k_cat = jnp.concatenate([k_buf[slot, base:base + half, :], k_buf[slot, base + half:base + 2 * half, :]], axis=1)
            s = lax.dot_general(qb_scr[rows[member]], k_cat, (((1,), (1,)), ((), ())), preferred_element_type=jnp.float32)
            scores.append(jnp.where(keep, s, -1e30))
        tops = []
        for s in scores:
            folded = jnp.maximum(s[:heads], s[heads:])
            tops.append(jnp.max(folded, axis=-1, keepdims=True))
        weights_in = [jnp.exp2((s - jnp.concatenate([top, top], axis=0)) * rate) for s, top in zip(scores, tops)]
        outs = []
        sums = []
        for member in range(GROUP):
            base = member * span_rows
            e = weights_in[member]
            sums.append(jnp.sum(e[:heads] + e[heads:], axis=-1, keepdims=True))
            v_cat = jnp.concatenate([v_buf[slot, base:base + half, :], v_buf[slot, base + half:base + 2 * half, :]], axis=1)
            both = jnp.dot(e.astype(jnp.bfloat16), v_cat, preferred_element_type=jnp.float32)
            outs.append(both[:heads, :head_dim] + both[heads:, head_dim:])
        for member in range(GROUP):
            row = rows[member]
            first = item_pos[group * GROUP + member] == 0
            run_max = jnp.where(first, s_scr[row], run_max)
            run_sum = jnp.where(first, 1.0, run_sum)
            run_out = jnp.where(first, v_scr[row], run_out)
            top = jnp.broadcast_to(tops[member], run_max.shape)
            new_max = jnp.maximum(run_max, top)
            keep_old = jnp.exp2((run_max - new_max) * rate)
            take_new = jnp.exp2((top - new_max) * rate)
            run_sum = run_sum * keep_old + take_new * sums[member]
            run_out = run_out * keep_old + take_new * outs[member]
            run_max = new_max
            o_scr[row] = run_out / run_sum
        return run_max, run_sum, run_out
    blank = jnp.zeros((heads, head_dim), jnp.float32)
    lax.fori_loop(0, groups, group_step, (blank, blank, blank))
    for head in range(heads):
        o_ref[:, head * head_dim:(head + 1) * head_dim] = o_scr[0:batch, head, :].astype(jnp.bfloat16)


def self_block(x, k_cache, v_cache, seq_lens, gain, bias, w_q, w_k, w_v):
    batch, width = x.shape
    ctx, heads, head_dim = k_cache.shape[1:]
    k_flat = k_cache.reshape(batch, ctx * heads, head_dim)
    v_flat = v_cache.reshape(batch, ctx * heads, head_dim)
    vmem = pl.BlockSpec(memory_space=pltpu.VMEM)
    hbm = pl.BlockSpec(memory_space=pl.ANY)
    flat = jax.ShapeDtypeStruct((batch, heads * head_dim), jnp.bfloat16)
    per_head = pltpu.VMEM((batch + 1, heads, head_dim), jnp.float32)
    kv_buf = pltpu.VMEM((KV_SLOTS, GROUP * SPAN * heads, head_dim), jnp.bfloat16)
    most_items = batch * ctx // SPAN + GROUP
    return pl.pallas_call(
        attn_kernel,
        out_shape=(flat, flat, flat),
        in_specs=[pl.BlockSpec(memory_space=pltpu.SMEM), vmem, vmem, vmem, hbm, hbm, hbm, hbm, hbm],
        out_specs=(vmem, vmem, vmem),
        scratch_shapes=[
            pltpu.VMEM((W_SLOTS, W_ROWS, heads * head_dim), jnp.bfloat16),
            kv_buf, kv_buf,
            pltpu.VMEM((width // W_ROWS, batch, W_ROWS), jnp.bfloat16),
            per_head,
            pltpu.VMEM((batch + 1, 2 * heads, 2 * head_dim), jnp.bfloat16),
            per_head, per_head, per_head, per_head,
            pltpu.VMEM((3, batch, heads * head_dim), jnp.float32),
            pltpu.SMEM((most_items,), jnp.int32),
            pltpu.SMEM((most_items,), jnp.int32),
            pltpu.SMEM((most_items,), jnp.int32),
            pltpu.SemaphoreType.DMA((W_SLOTS,)),
            pltpu.SemaphoreType.DMA((KV_SLOTS,)),
            pltpu.SemaphoreType.DMA((KV_SLOTS,)),
        ],
        compiler_params=pltpu.CompilerParams(vmem_limit_bytes=60 * 1024 * 1024),
        name='self_block',
    )(seq_lens, x, gain.reshape(1, width), bias.reshape(1, width), w_q, w_k, w_v, k_flat, v_flat)


RING = 15
CUT = 256
QUAD = 512
SIDE = 1024


def mix_kernel(x_ref, o_ref, g2_ref, b2_ref, g3_ref, b3_ref, enc_ref, wo_ref, wq_ref, wk_ref, wv_ref, woc_ref, wup_ref, wdn_ref,
               out_ref,
               ring, e_buf, w_all, v_own, lhs, acc, h_scr, q_scr, q_send, q_recv, d_scr, p_scr, st_send, st_recv, o_mine, o_send, o_recv,
               ar_part, ar_half, ar_r1, ar_r2, ar_tot,
               ring_sem, e_sem, w_sem, ex_send, ex_recv, x_send, x_recv, y_send, y_recv, ar_send, ar_recv):
    batch, width = x_ref.shape
    head_dim = 128
    rate = head_dim ** -0.5 * LOG2_E
    dp = lax.axis_index('dp')
    tp = lax.axis_index('tp')
    core = lax.rem(tp, 2)
    mate = tp + 1 - 2 * core
    across = lax.rem(tp + 2, 4)
    other = 1 - dp
    to_mate, to_across, to_other = {'tp': mate}, {'tp': across}, {'dp': other}
    mesh_id = pl.DeviceIdType.MESH
    tokens = enc_ref.shape[1]
    spans = batch // 4

    barrier = pltpu.get_barrier_semaphore()
    for peer in (to_mate, to_across, to_other):
        pl.semaphore_signal(barrier, inc=1, device_id=peer, device_id_type=mesh_id)

    segments = ((wo_ref, 0, 4, False), (wq_ref, 4, 8, True), (woc_ref, 8, 12, False), (wup_ref, 12, 28, False), (wdn_ref, 28, 44, False))

    def ring_copy(src, deep, row, slot, piece):
        if deep:
            view = src.at[pl.ds(row * SIDE + piece * CUT, CUT), :]
        else:
            view = src.at[pl.ds(row * CUT, CUT), pl.ds(piece * SIDE, SIDE)]
        return pltpu.make_async_copy(view, ring.at[slot, piece], ring_sem.at[slot, piece])

    def ring_start(index):
        for src, low, high, deep in segments:
            @pl.when((index >= low) & (index < high))
            def _():
                for piece in range(4):
                    ring_copy(src, deep, index - low, lax.rem(index, RING), piece).start()

    def ring_wait(index):
        slot = lax.rem(index, RING)
        for piece in range(4):
            ring_copy(wo_ref, False, 0, slot, piece).wait()
        return slot

    def stream_wide(base, count):
        acc[...] = jnp.zeros_like(acc)

        def step(chunk, carry):
            slot = ring_wait(base + chunk)
            for piece in range(4):
                acc[piece] += jnp.dot(lhs[chunk], ring[slot, piece], preferred_element_type=jnp.float32)
            ring_start(base + chunk + RING)
            return carry
        lax.fori_loop(0, count, step, 0)

    for index in range(4):
        for piece in range(4):
            ring_copy(wo_ref, False, index, index, piece).start()
    mine = pl.ds(pl.multiple_of(core * tokens, tokens), tokens)
    e_local = pltpu.make_async_copy(enc_ref, e_buf.at[:, mine, :], e_sem)
    e_local.start()
    own_copies = []
    for kind, src in ((1, wv_ref), (0, wk_ref)):
        for quad in range(2):
            copy = pltpu.make_async_copy(src.at[:, pl.ds(quad * QUAD, QUAD)], w_all.at[kind, 0, quad], w_sem.at[kind, quad])
            copy.start()
            own_copies.append(copy)
    pl.semaphore_wait(barrier, 3)
    e_remote = pltpu.make_async_remote_copy(src_ref=enc_ref, dst_ref=e_buf.at[:, mine, :], send_sem=ex_send.at[0], recv_sem=ex_recv.at[0], device_id=to_mate, device_id_type=mesh_id)
    e_remote.start()

    def x_copy(unit):
        kind, column = unit // 4, unit % 4 * head_dim
        src = (wk_ref, wv_ref)[kind]
        start = pl.multiple_of(dp * QUAD + column, head_dim)
        return pltpu.make_async_remote_copy(src_ref=src.at[:, pl.ds(start, head_dim)], dst_ref=w_all.at[kind, 1, dp, :, pl.ds(column, head_dim)],
                                            send_sem=x_send.at[unit], recv_sem=x_recv.at[unit], device_id=to_across, device_id_type=mesh_id)

    def y_copy(unit):
        kind, column = unit // 4, unit % 4 * head_dim
        view = w_all.at[kind, 1, dp, :, pl.ds(column, head_dim)]
        return pltpu.make_async_remote_copy(src_ref=view, dst_ref=view, send_sem=y_send.at[unit], recv_sem=y_recv.at[unit], device_id=to_other, device_id_type=mesh_id)

    def relay(unit):
        x_copy(unit).wait_recv()
        y_copy(unit).start()

    for unit in range(8):
        x_copy(unit).start()
    for index in range(4, RING):
        ring_start(jnp.int32(index))

    def ar_copy(which, stage):
        if stage == 0:
            return pltpu.make_async_remote_copy(src_ref=ar_part.at[1 - core], dst_ref=ar_r1.at[which], send_sem=ar_send.at[which, 0], recv_sem=ar_recv.at[which, 0], device_id=to_mate, device_id_type=mesh_id)
        if stage == 1:
            return pltpu.make_async_remote_copy(src_ref=ar_half, dst_ref=ar_r2.at[which], send_sem=ar_send.at[which, 1], recv_sem=ar_recv.at[which, 1], device_id=to_across, device_id_type=mesh_id)
        return pltpu.make_async_remote_copy(src_ref=ar_tot.at[which, core], dst_ref=ar_tot.at[which, core], send_sem=ar_send.at[which, 2], recv_sem=ar_recv.at[which, 2], device_id=to_mate, device_id_type=mesh_id)

    def reduce_open(which):
        for half in range(2):
            for piece in range(2):
                ar_part[half, :, piece * SIDE:(piece + 1) * SIDE] = acc[half * 2 + piece].astype(jnp.bfloat16)
        ar_copy(which, 0).start()
        ar_copy(which, 0).wait()
        ar_half[...] = (ar_part[core].astype(jnp.float32) + ar_r1[which].astype(jnp.float32)).astype(jnp.bfloat16)
        ar_copy(which, 1).start()

    def reduce_close(which):
        ar_copy(which, 1).wait()
        ar_tot[which, core] = (ar_half[...].astype(jnp.float32) + ar_r2[which].astype(jnp.float32)).astype(jnp.bfloat16)
        ar_copy(which, 2).start()
        ar_copy(which, 2).wait()

    def total(which):
        return jnp.concatenate([ar_tot[which, 0].astype(jnp.float32), ar_tot[which, 1].astype(jnp.float32)], axis=1)

    def norm_into_lhs(values, gain_ref, bias_ref):
        row_mean = jnp.mean(values, axis=-1, keepdims=True)
        centred = values - row_mean
        row_var = jnp.mean(jnp.square(centred), axis=-1, keepdims=True)
        normed = (centred * lax.rsqrt(row_var + LN_EPS) * gain_ref[...] + bias_ref[...]).astype(jnp.bfloat16)
        for chunk in range(width // CUT):
            lhs[chunk] = normed[:, chunk * CUT:(chunk + 1) * CUT]

    def project_span(kind, side, quad, span):
        tile = e_buf[pl.ds(span * 4, 4)].reshape(4 * 2 * tokens, e_buf.shape[2])
        return jnp.dot(tile, w_all[kind, side, quad], preferred_element_type=jnp.float32).astype(jnp.bfloat16)

    row_id = lax.broadcasted_iota(jnp.int32, (16, QUAD), 0)
    col_tile = lax.broadcasted_iota(jnp.int32, (16, QUAD), 1) // head_dim
    head_match = row_id // 4 == col_tile
    seq_match = lax.rem(row_id, 4) == col_tile

    def keys_and_scores(side, quad):
        def step(span, carry):
            keys = project_span(0, side, quad, span)
            q4 = q_scr[side, quad, span]
            rows = jnp.where(head_match, jnp.concatenate([q4, q4, q4, q4], axis=0), 0.0).astype(jnp.bfloat16)
            s = lax.dot_general(rows, keys, (((1,), (1,)), ((), ())), preferred_element_type=jnp.float32)
            s = jnp.where(seq_match, s, 0.0)
            d_scr[side, quad, span] = s[:, 0:128] + s[:, 128:256] + s[:, 256:384] + s[:, 384:512]
            return carry
        lax.fori_loop(0, spans, step, 0, unroll=2)

    def own_values(quad):
        def step(span, carry):
            v_own[quad, span] = project_span(1, 0, quad, span)
            return carry
        lax.fori_loop(0, spans, step, 0, unroll=2)

    def apply_weights(side, quad, dest):
        def step(span, carry):
            values = v_own[quad, span] if side == 0 else project_span(1, side, quad, span)
            p = p_scr[side, quad, span]
            rows = jnp.where(seq_match, jnp.concatenate([p, p, p, p], axis=1), 0.0).astype(jnp.bfloat16)
            wide = jnp.dot(rows, values, preferred_element_type=jnp.float32)
            wide = jnp.where(head_match, wide, 0.0)
            dest[quad, span] = wide[0:4] + wide[4:8] + wide[8:12] + wide[12:16]
            return carry
        lax.fori_loop(0, spans, step, 0, unroll=2)

    for chunk in range(4):
        lhs[chunk] = o_ref[:, chunk * CUT:(chunk + 1) * CUT]
    stream_wide(0, 4)
    reduce_open(0)
    e_local.wait()
    e_remote.wait()
    own_copies[0].wait()
    own_values(0)
    relay(0)
    reduce_close(0)
    h_one = x_ref[...].astype(jnp.float32) + total(0)
    h_scr[...] = h_one
    norm_into_lhs(h_one, g2_ref, b2_ref)

    def query_step(chunk, carry):
        slot = ring_wait(4 + chunk)
        for piece in range(4):
            acc[0] += jnp.dot(lhs[chunk * 4 + piece], ring[slot, piece], preferred_element_type=jnp.float32)
        ring_start(4 + chunk + RING)
        return carry
    acc[0] = jnp.zeros_like(acc[0])
    lax.fori_loop(0, 4, query_step, 0)
    q_new = acc[0].astype(jnp.bfloat16)
    q_send[...] = q_new
    q_copy = pltpu.make_async_remote_copy(src_ref=q_send, dst_ref=q_recv, send_sem=ex_send.at[1], recv_sem=ex_recv.at[1], device_id=to_across, device_id_type=mesh_id)
    q_copy.start()
    relay(1)

    def spread_query(side, q):
        wide = q.astype(jnp.float32)
        for quad in range(2):
            for span in range(spans):
                q_scr[side, quad, span] = wide[span * 4:span * 4 + 4, quad * QUAD:(quad + 1) * QUAD]
    spread_query(0, q_new)
    own_copies[1].wait()
    own_values(1)
    relay(2)
    own_copies[2].wait()
    own_copies[3].wait()
    keys_and_scores(0, 0)
    relay(3)
    keys_and_scores(0, 1)
    relay(4)
    q_copy.wait()
    spread_query(1, q_recv[...])
    keys_and_scores(1, dp)
    relay(5)
    for unit in range(4):
        y_copy(unit).wait_recv()
    keys_and_scores(1, other)
    relay(6)

    lane = lax.broadcasted_iota(jnp.int32, (128, 128), 1)

    def block_stats(side, quad):
        s = d_scr[side, quad].reshape(128, 128)
        top = jnp.max(s, axis=-1, keepdims=True)
        part = jnp.sum(jnp.exp2((s - top) * rate), axis=-1, keepdims=True)
        return s, top, part

    for side in range(2):
        for quad in range(2):
            s, top, part = block_stats(side, quad)
            packed = jnp.where(lane == 0, top, jnp.where(lane == 1, part, 0.0))
            st_send[side, quad] = packed.T[0:8, :]
    st_copy = pltpu.make_async_remote_copy(src_ref=st_send, dst_ref=st_recv, send_sem=ex_send.at[2], recv_sem=ex_recv.at[2], device_id=to_across, device_id_type=mesh_id)
    st_copy.start()
    relay(7)
    st_copy.wait()
    for side in range(2):
        for quad in range(2):
            s, top, part = block_stats(side, quad)
            theirs = jnp.concatenate([st_recv[1 - side, quad], jnp.zeros((120, 128), jnp.float32)], axis=0).T
            their_top, their_part = theirs[:, 0:1], theirs[:, 1:2]
            whole_top = jnp.maximum(top, their_top)
            whole = part * jnp.exp2((top - whole_top) * rate) + their_part * jnp.exp2((their_top - whole_top) * rate)
            p = jnp.exp2((s - whole_top) * rate) / whole
            p_scr[side, quad] = p.reshape(8, 16, 128)
    apply_weights(0, 0, o_mine)
    apply_weights(0, 1, o_mine)

    def o_copy(slot, quad):
        return pltpu.make_async_remote_copy(src_ref=o_send.at[quad], dst_ref=o_recv.at[quad], send_sem=ex_send.at[3 + slot], recv_sem=ex_recv.at[3 + slot], device_id=to_across, device_id_type=mesh_id)
    apply_weights(1, dp, o_send)
    o_copy(0, dp).start()
    for unit in range(4, 8):
        y_copy(unit).wait_recv()
    apply_weights(1, other, o_send)
    o_copy(1, other).start()
    o_copy(0, dp).wait()
    o_copy(1, other).wait()
    for quad in range(2):
        whole = o_mine[quad] + o_recv[quad]
        whole = jnp.concatenate([whole[span] for span in range(spans)], axis=0).astype(jnp.bfloat16)
        for piece in range(2):
            lhs[quad * 2 + piece] = whole[:, piece * CUT:(piece + 1) * CUT]
    stream_wide(8, 4)
    reduce_open(1)
    reduce_close(1)
    h_two = h_scr[...] + total(1)
    h_scr[...] = h_two
    norm_into_lhs(h_two, g3_ref, b3_ref)
    stream_wide(12, 16)
    for piece in range(4):
        u = acc[piece]
        u = (0.5 * u * (1.0 + lax.erf(u * (0.5 ** 0.5)))).astype(jnp.bfloat16)
        for chunk in range(4):
            lhs[piece * 4 + chunk] = u[:, chunk * CUT:(chunk + 1) * CUT]
    stream_wide(28, 16)
    reduce_open(2)
    for unit in range(8):
        x_copy(unit).wait_send()
        y_copy(unit).wait_send()
    reduce_close(2)
    out_ref[...] = (h_scr[...] + total(2)).astype(jnp.bfloat16)


def mix_block(x, self_out, nbr_enc, ln2_gain, ln2_bias, wq_c, wk_c, wv_c, w_o, wo_c, ln3_gain, ln3_bias, w_up, w_down):
    batch, width = x.shape
    _, tokens, enc = nbr_enc.shape
    vmem = pl.BlockSpec(memory_space=pltpu.VMEM)
    hbm = pl.BlockSpec(memory_space=pl.ANY)
    spans = batch // 4
    bf, f32 = jnp.bfloat16, jnp.float32
    dma = pltpu.SemaphoreType.DMA
    half = width // 2
    return pl.pallas_call(
        mix_kernel,
        out_shape=jax.ShapeDtypeStruct((batch, width), bf),
        in_specs=[vmem] * 6 + [hbm] * 8,
        out_specs=vmem,
        scratch_shapes=[
            pltpu.VMEM((RING, 4, CUT, SIDE), bf),
            pltpu.VMEM((batch, 2 * tokens, enc), bf),
            pltpu.VMEM((2, 2, 2, enc, QUAD), bf),
            pltpu.VMEM((2, spans, 8 * tokens, QUAD), bf),
            pltpu.VMEM((width // CUT, batch, CUT), bf),
            pltpu.VMEM((4, batch, SIDE), f32),
            pltpu.VMEM((batch, width), f32),
            pltpu.VMEM((2, 2, spans, 4, QUAD), f32),
            pltpu.VMEM((batch, SIDE), bf),
            pltpu.VMEM((batch, SIDE), bf),
            pltpu.VMEM((2, 2, spans, 16, 128), f32),
            pltpu.VMEM((2, 2, spans, 16, 128), f32),
            pltpu.VMEM((2, 2, 8, 128), f32),
            pltpu.VMEM((2, 2, 8, 128), f32),
            pltpu.VMEM((2, spans, 4, QUAD), f32),
            pltpu.VMEM((2, spans, 4, QUAD), f32),
            pltpu.VMEM((2, spans, 4, QUAD), f32),
            pltpu.VMEM((2, batch, half), bf),
            pltpu.VMEM((batch, half), bf),
            pltpu.VMEM((3, batch, half), bf),
            pltpu.VMEM((3, batch, half), bf),
            pltpu.VMEM((3, 2, batch, half), bf),
            dma((RING, 4)), dma, dma((2, 2)), dma((5,)), dma((5,)), dma((8,)), dma((8,)), dma((8,)), dma((8,)), dma((3, 3)), dma((3, 3)),
        ],
        compiler_params=pltpu.CompilerParams(vmem_limit_bytes=67043328, collective_id=0, has_side_effects=True),
        name='mix_block',
    )(x, self_out, ln2_gain.reshape(1, width), ln2_bias.reshape(1, width), ln3_gain.reshape(1, width), ln3_bias.reshape(1, width), nbr_enc, w_o, wq_c, wk_c, wv_c, wo_c, w_up, w_down)


def local_step(x, k_cache, v_cache, seq_lens, nbr_enc, ln1_gain, ln1_bias, w_q, w_k, w_v, w_o, ln2_gain, ln2_bias, wq_c, wk_c, wv_c, wo_c, ln3_gain, ln3_bias, w_up, w_down):
    batch = x.shape[0]
    heads, head_dim = k_cache.shape[2:]
    self_out, k_new, v_new = self_block(x, k_cache, v_cache, seq_lens, ln1_gain, ln1_bias, w_q, w_k, w_v)
    layer_out = mix_block(x, self_out, nbr_enc, ln2_gain, ln2_bias, wq_c, wk_c, wv_c, w_o, wo_c, ln3_gain, ln3_bias, w_up, w_down)
    return layer_out, k_new.reshape(batch, heads, head_dim), v_new.reshape(batch, heads, head_dim)


def solution(mesh):
    row_spec = P('dp', None)
    cache_spec = P('dp', None, 'tp', None)
    head_spec = P('dp', 'tp', None)
    vec_spec = P(None)
    col_split = P(None, 'tp')
    row_split = P('tp', None)
    in_specs = (row_spec, cache_spec, cache_spec, P('dp'), P('dp', 'tp', None), vec_spec, vec_spec, col_split, col_split, col_split, row_split, vec_spec, vec_spec, col_split, col_split, col_split, row_split, vec_spec, vec_spec, col_split, row_split)
    out_specs = (row_spec, head_spec, head_spec)
    return jax.shard_map(local_step, mesh=mesh, in_specs=in_specs, out_specs=out_specs, check_vma=False)
```

time: 397 us -> 179 us (0.45); the launches traced: 393 us -> 181 us
  matrix products: 175 us -> 0 us
  Pallas kernels: 0 us -> 175 us
  waiting for transfers between devices: 169 us -> 0 us
  local copies, waits for them, and re-layouts: 23.3 us -> 4.63 us
  between operations: 14.3 us -> 0.65 us
  other arithmetic: 10.8 us -> 0 us
    pallas_call x0 -> x2, Pallas kernels: none -> 175 us  [the longest x1 140 us: mix_block(): pl.pallas_call(mix_kernel, out_shape=jax.ShapeDtypeStruct((batch, width),...]
    dot_general x13 -> x0, matrix products: 175 us -> none  [the longest x7 57.1 us: project(): jnp.dot(operand, weight, preferred_element_type=jnp.float32)]
    all_gather x1 -> x0, waiting for transfers between devices: 86.2 us -> none  [local_step(): enc_all = lax.all_gather(nbr_enc, 'tp', axis=1, tiled=True)]
    psum x3 -> x0, waiting for transfers between devices: 81.8 us -> none  [the longest x1 28.6 us: local_step(): residual = residual + lax.psum(self_part, 'tp').astype(jnp.float32)]
    reshape x3 -> x0, local copies, waits for them, and re-layouts: 22.6 us -> none  [the longest x1 22.5 us: local_step(): jnp.einsum('bne,ef->bnf', enc_all, wk_c, preferred_element_type=jnp.float32)]
    reduce_sum x7 -> x0, other arithmetic: 7.56 us -> none  [the longest x3 3.58 us: layer_norm(): row_var = jnp.mean(jnp.square(centred), axis=-1, keepdims=True)]
    unnamed x31 -> x3, local copies, waits for them, and re-layouts: 0.65 us -> 4.63 us
  transfers between devices with their start and end apart: 4 -> 0, of which waited for: 4 -> 0; matrix products, arithmetic and copies ran while one was open for 2% -> 0% of each run, Pallas kernels for 0% -> 0%
where the time goes in v1:
time: 179 us; the launch traced here: 181 us
  Pallas kernels  175 us (98%)
  local copies, waits for them, and re-layouts  4.63 us (3%)
    pallas_call x1, Pallas kernels, mix_block(): pl.pallas_call(mix_kernel, out_shape=jax.ShapeDtypeStruct((batch, width),...  140 us
    pallas_call x1, Pallas kernels, self_block(): pl.pallas_call(attn_kernel, out_shape=(flat, flat, flat), in_specs=[pl.Bl...  35.6 us
    unnamed x3, local copies, waits for them, and re-layouts  4.63 us

profile of v1, /device:TPU:0, one launch (start us, length us, event | category | flops | bytes accessed | tf_op | source)
XLA Modules:
  0.0 180.5 jit_solution(9005563317720296490)
XLA Ops:
  0.6 35.6 %self_block.1 = (bf16[32,1024]{1,0:T(8,128)(2,1)}, bf16[32,1024]{1,0:T(8,128)(2,1)}, bf16[32,1024]{1,0:T(8,128)(2,1)}) custom-call(s32[32]{0:T(128)} %lens_ref.1, bf16[32,4096]{1,0:T(8,128)(2,1)} %x_ref.3, f32[1,4096]{1,0:T(1,128)} %bitcast.16, f32[1,4096]{1,0:T(1,128)} %bitcast.17, bf16[4096,1024]{1,0:T(8,128)(2,1)} %wq_ref.2, bf16[4096,1024]{1,0:T(8,128)(2,1)} %wk_ref.2, ...), custom_call_target="tpu_custom_call" | custom-call | tf_op jit(solution)/shard_map/self_block/pallas_call | solution.py:177
  36.3 1.5 copy.24
  37.8 1.5 copy.25
  39.2 139.6 %mix_block.1 = bf16[32,4096]{1,0:T(8,128)(2,1)} custom-call(bf16[32,4096]{1,0:T(8,128)(2,1)} %x_ref.3, bf16[32,1024]{1,0:T(8,128)(2,1)} %get-tuple-element.6.o_ref, f32[1,4096]{1,0:T(1,128)} %bitcast.18, f32[1,4096]{1,0:T(1,128)} %bitcast.19, f32[1,4096]{1,0:T(1,128)} %bitcast.20, f32[1,4096]{1,0:T(1,128)} %bitcast.21, bf16[32,64,896]{2,1,0:T(8,128)(2,1)} %enc_ref.1, ...), custom_call_target="tpu_custom_call" | custom-call | tf_op jit(solution)/shard_map/mix_block/pallas_call | solution.py:497
  178.8 1.7 copy.27

commit v2 on v1

--- a/solution.py
+++ b/solution.py
@@ -10,8 +10,8 @@
 W_SLOTS = 8
 W_ROWS = 512
 SPAN = 64
-GROUP = 8
-KV_SLOTS = 5
+GROUP = 12
+KV_SLOTS = 4
 
 
 def attn_kernel(lens_ref, x_ref, g_ref, b_ref, wq_ref, wk_ref, wv_ref, kc_ref, vc_ref,
@@ -87,14 +87,13 @@
 
     for which in range(3):
         out = acc_scr[which].astype(jnp.bfloat16)
-        if which == 1:
-            kn_ref[...] = out
-        if which == 2:
-            vn_ref[...] = out
         rounded = out.astype(jnp.float32)
         dest = (q_scr, k_scr, v_scr)[which]
         for head in range(heads):
             dest[0:batch, head, :] = rounded[:, head * head_dim:(head + 1) * head_dim]
+
+    kn_ref[...] = k_scr[0:batch].astype(jnp.bfloat16)
+    vn_ref[...] = v_scr[0:batch].astype(jnp.bfloat16)
 
     def prepare(row, carry):
         q = q_scr[row]
@@ -171,12 +170,13 @@
     vmem = pl.BlockSpec(memory_space=pltpu.VMEM)
     hbm = pl.BlockSpec(memory_space=pl.ANY)
     flat = jax.ShapeDtypeStruct((batch, heads * head_dim), jnp.bfloat16)
+    new = jax.ShapeDtypeStruct((batch, heads, head_dim), jnp.bfloat16)
     per_head = pltpu.VMEM((batch + 1, heads, head_dim), jnp.float32)
     kv_buf = pltpu.VMEM((KV_SLOTS, GROUP * SPAN * heads, head_dim), jnp.bfloat16)
     most_items = batch * ctx // SPAN + GROUP
     return pl.pallas_call(
         attn_kernel,
-        out_shape=(flat, flat, flat),
+        out_shape=(flat, new, new),
         in_specs=[pl.BlockSpec(memory_space=pltpu.SMEM), vmem, vmem, vmem, hbm, hbm, hbm, hbm, hbm],
         out_specs=(vmem, vmem, vmem),
         scratch_shapes=[
@@ -195,21 +195,23 @@
             pltpu.SemaphoreType.DMA((KV_SLOTS,)),
         ],
         compiler_params=pltpu.CompilerParams(vmem_limit_bytes=60 * 1024 * 1024),
+        cost_estimate=pl.CostEstimate(flops=100_000_000_000, bytes_accessed=100_000_000, transcendentals=0),
         name='self_block',
     )(seq_lens, x, gain.reshape(1, width), bias.reshape(1, width), w_q, w_k, w_v, k_flat, v_flat)
 
 
 RING = 15
+LATE = 4
 CUT = 256
 QUAD = 512
 SIDE = 1024
 
 
-def mix_kernel(x_ref, o_ref, g2_ref, b2_ref, g3_ref, b3_ref, enc_ref, wo_ref, wq_ref, wk_ref, wv_ref, woc_ref, wup_ref, wdn_ref,
+def mix_kernel(x_ref, o_ref, g2_ref, b2_ref, g3_ref, b3_ref, enc_ref, encm_ref, wkx_ref, wvx_ref, wo_ref, wq_ref, wk_ref, wv_ref, woc_ref, wup_ref, wdn_ref,
                out_ref,
-               ring, e_buf, w_all, v_own, lhs, acc, h_scr, q_scr, q_send, q_recv, d_scr, p_scr, st_send, st_recv, o_mine, o_send, o_recv,
+               ring, e_buf, w_all, lhs, acc, h_scr, q_scr, q_send, q_recv, d_scr, p_scr, st_send, st_recv, o_mine, o_send, o_recv,
                ar_part, ar_half, ar_r1, ar_r2, ar_tot,
-               ring_sem, e_sem, w_sem, ex_send, ex_recv, x_send, x_recv, y_send, y_recv, ar_send, ar_recv):
+               ring_sem, e_sem, w_sem, x_sem, ex_send, ex_recv, y_send, y_recv, ar_send, ar_recv):
     batch, width = x_ref.shape
     head_dim = 128
     rate = head_dim ** -0.5 * LOG2_E
@@ -228,7 +230,7 @@
     for peer in (to_mate, to_across, to_other):
         pl.semaphore_signal(barrier, inc=1, device_id=peer, device_id_type=mesh_id)
 
-    segments = ((wo_ref, 0, 4, False), (wq_ref, 4, 8, True), (woc_ref, 8, 12, False), (wup_ref, 12, 28, False), (wdn_ref, 28, 44, False))
+    segments = ((wo_ref, 0, 4, False), (wq_ref, 4, 8, True), (woc_ref, 8, 12, False), (wup_ref, 12, 28, False), (wdn_ref, 28, 44 - LATE, False))
 
     def ring_copy(src, deep, row, slot, piece):
         if deep:
@@ -244,59 +246,69 @@
                 for piece in range(4):
                     ring_copy(src, deep, index - low, lax.rem(index, RING), piece).start()
 
+    def slot_wait(slot):
+        for piece in range(4):
+            ring_copy(wo_ref, False, 0, slot, piece).wait()
+
     def ring_wait(index):
         slot = lax.rem(index, RING)
-        for piece in range(4):
-            ring_copy(wo_ref, False, 0, slot, piece).wait()
+        slot_wait(slot)
         return slot
 
-    def stream_wide(base, count):
+    def stream_wide(base, count, refill=True):
         acc[...] = jnp.zeros_like(acc)
 
         def step(chunk, carry):
             slot = ring_wait(base + chunk)
             for piece in range(4):
                 acc[piece] += jnp.dot(lhs[chunk], ring[slot, piece], preferred_element_type=jnp.float32)
-            ring_start(base + chunk + RING)
+            if refill:
+                ring_start(base + chunk + RING)
             return carry
         lax.fori_loop(0, count, step, 0)
+
+    def late_start():
+        for late in range(LATE):
+            for piece in range(4):
+                ring_copy(wdn_ref, False, 16 - LATE + late, RING + late, piece).start()
+
+    def late_finish():
+        def step(late, carry):
+            slot_wait(RING + late)
+            for piece in range(4):
+                acc[piece] += jnp.dot(lhs[16 - LATE + late], ring[RING + late, piece], preferred_element_type=jnp.float32)
+            return carry
+        lax.fori_loop(0, LATE, step, 0)
 
     for index in range(4):
         for piece in range(4):
             ring_copy(wo_ref, False, index, index, piece).start()
     mine = pl.ds(pl.multiple_of(core * tokens, tokens), tokens)
-    e_local = pltpu.make_async_copy(enc_ref, e_buf.at[:, mine, :], e_sem)
+    theirs_at = pl.ds(pl.multiple_of((1 - core) * tokens, tokens), tokens)
+    e_local = pltpu.make_async_copy(enc_ref, e_buf.at[:, mine, :], e_sem.at[0])
     e_local.start()
+    e_mate = pltpu.make_async_copy(encm_ref, e_buf.at[:, theirs_at, :], e_sem.at[1])
+    e_mate.start()
     own_copies = []
     for kind, src in ((1, wv_ref), (0, wk_ref)):
         for quad in range(2):
-            copy = pltpu.make_async_copy(src.at[:, pl.ds(quad * QUAD, QUAD)], w_all.at[kind, 0, quad], w_sem.at[kind, quad])
-            copy.start()
+            copy = pltpu.make_async_copy(src.at[:, pl.ds(quad * QUAD, QUAD)], w_all.at[kind, 0, :, pl.ds(quad * QUAD, QUAD)], w_sem.at[kind, quad])
+            if kind == 1:
+                copy.start()
             own_copies.append(copy)
     pl.semaphore_wait(barrier, 3)
-    e_remote = pltpu.make_async_remote_copy(src_ref=enc_ref, dst_ref=e_buf.at[:, mine, :], send_sem=ex_send.at[0], recv_sem=ex_recv.at[0], device_id=to_mate, device_id_type=mesh_id)
-    e_remote.start()
-
-    def x_copy(unit):
-        kind, column = unit // 4, unit % 4 * head_dim
-        src = (wk_ref, wv_ref)[kind]
-        start = pl.multiple_of(dp * QUAD + column, head_dim)
-        return pltpu.make_async_remote_copy(src_ref=src.at[:, pl.ds(start, head_dim)], dst_ref=w_all.at[kind, 1, dp, :, pl.ds(column, head_dim)],
-                                            send_sem=x_send.at[unit], recv_sem=x_recv.at[unit], device_id=to_across, device_id_type=mesh_id)
-
-    def y_copy(unit):
-        kind, column = unit // 4, unit % 4 * head_dim
-        view = w_all.at[kind, 1, dp, :, pl.ds(column, head_dim)]
-        return pltpu.make_async_remote_copy(src_ref=view, dst_ref=view, send_sem=y_send.at[unit], recv_sem=y_recv.at[unit], device_id=to_other, device_id_type=mesh_id)
-
-    def relay(unit):
-        x_copy(unit).wait_recv()
-        y_copy(unit).start()
-
-    for unit in range(8):
-        x_copy(unit).start()
-    for index in range(4, RING):
-        ring_start(jnp.int32(index))
+    half_rows = wkx_ref.shape[0]
+    crossed = (wkx_ref, wvx_ref)
+    here = pl.ds(pl.multiple_of(dp * half_rows, half_rows), half_rows)
+
+    def x_copy(kind):
+        return pltpu.make_async_copy(crossed[kind], w_all.at[kind, 1, here, :], x_sem.at[kind])
+
+    def y_copy(kind):
+        return pltpu.make_async_remote_copy(src_ref=crossed[kind], dst_ref=w_all.at[kind, 1, here, :], send_sem=y_send.at[kind], recv_sem=y_recv.at[kind], device_id=to_other, device_id_type=mesh_id)
+
+    for kind in range(2):
+        y_copy(kind).start()
 
     def ar_copy(which, stage):
         if stage == 0:
@@ -305,19 +317,23 @@
             return pltpu.make_async_remote_copy(src_ref=ar_half, dst_ref=ar_r2.at[which], send_sem=ar_send.at[which, 1], recv_sem=ar_recv.at[which, 1], device_id=to_across, device_id_type=mesh_id)
         return pltpu.make_async_remote_copy(src_ref=ar_tot.at[which, core], dst_ref=ar_tot.at[which, core], send_sem=ar_send.at[which, 2], recv_sem=ar_recv.at[which, 2], device_id=to_mate, device_id_type=mesh_id)
 
-    def reduce_open(which):
+    def nothing():
+        return None
+
+    def reduce(which, first=nothing, second=nothing, third=nothing):
         for half in range(2):
             for piece in range(2):
                 ar_part[half, :, piece * SIDE:(piece + 1) * SIDE] = acc[half * 2 + piece].astype(jnp.bfloat16)
         ar_copy(which, 0).start()
+        first()
         ar_copy(which, 0).wait()
         ar_half[...] = (ar_part[core].astype(jnp.float32) + ar_r1[which].astype(jnp.float32)).astype(jnp.bfloat16)
         ar_copy(which, 1).start()
-
-    def reduce_close(which):
+        second()
         ar_copy(which, 1).wait()
         ar_tot[which, core] = (ar_half[...].astype(jnp.float32) + ar_r2[which].astype(jnp.float32)).astype(jnp.bfloat16)
         ar_copy(which, 2).start()
+        third()
         ar_copy(which, 2).wait()
 
     def total(which):
@@ -333,7 +349,7 @@
 
     def project_span(kind, side, quad, span):
         tile = e_buf[pl.ds(span * 4, 4)].reshape(4 * 2 * tokens, e_buf.shape[2])
-        return jnp.dot(tile, w_all[kind, side, quad], preferred_element_type=jnp.float32).astype(jnp.bfloat16)
+        return jnp.dot(tile, w_all[kind, side, :, quad * QUAD:(quad + 1) * QUAD], preferred_element_type=jnp.float32).astype(jnp.bfloat16)
 
     row_id = lax.broadcasted_iota(jnp.int32, (16, QUAD), 0)
     col_tile = lax.broadcasted_iota(jnp.int32, (16, QUAD), 1) // head_dim
@@ -349,35 +365,52 @@
             s = jnp.where(seq_match, s, 0.0)
             d_scr[side, quad, span] = s[:, 0:128] + s[:, 128:256] + s[:, 256:384] + s[:, 384:512]
             return carry
-        lax.fori_loop(0, spans, step, 0, unroll=2)
-
-    def own_values(quad):
+        lax.fori_loop(0, spans, step, 0, unroll=4)
+
+    def own_values(quad, low, high):
         def step(span, carry):
-            v_own[quad, span] = project_span(1, 0, quad, span)
+            values = project_span(1, 0, quad, span)
+            slot, piece = RING + quad * 2 + span // 4, span % 4
+            ring[slot, piece, :, 0:QUAD] = values[0:CUT]
+            ring[slot, piece, :, QUAD:SIDE] = values[CUT:2 * CUT]
             return carry
-        lax.fori_loop(0, spans, step, 0, unroll=2)
+        lax.fori_loop(low, high, step, 0, unroll=2)
+
+    def own_tile(quad, span):
+        tile = ring[RING + quad * 2 + span // 4, span % 4]
+        return jnp.concatenate([tile[:, 0:QUAD], tile[:, QUAD:SIDE]], axis=0)
 
     def apply_weights(side, quad, dest):
         def step(span, carry):
-            values = v_own[quad, span] if side == 0 else project_span(1, side, quad, span)
+            values = own_tile(quad, span) if side == 0 else project_span(1, side, quad, span)
             p = p_scr[side, quad, span]
             rows = jnp.where(seq_match, jnp.concatenate([p, p, p, p], axis=1), 0.0).astype(jnp.bfloat16)
             wide = jnp.dot(rows, values, preferred_element_type=jnp.float32)
             wide = jnp.where(head_match, wide, 0.0)
             dest[quad, span] = wide[0:4] + wide[4:8] + wide[8:12] + wide[12:16]
             return carry
-        lax.fori_loop(0, spans, step, 0, unroll=2)
+        lax.fori_loop(0, spans, step, 0, unroll=4)
 
     for chunk in range(4):
         lhs[chunk] = o_ref[:, chunk * CUT:(chunk + 1) * CUT]
-    stream_wide(0, 4)
-    reduce_open(0)
-    e_local.wait()
-    e_remote.wait()
-    own_copies[0].wait()
-    own_values(0)
-    relay(0)
-    reduce_close(0)
+    stream_wide(0, 4, refill=False)
+    for index in range(4, 8):
+        ring_start(jnp.int32(index))
+    for copy in own_copies[2:]:
+        copy.start()
+    for kind in range(2):
+        x_copy(kind).start()
+
+    def open_values():
+        e_local.wait()
+        e_mate.wait()
+        own_copies[0].wait()
+        own_values(0, 0, 2)
+
+    def more_values():
+        own_copies[1].wait()
+        own_values(1, 0, 2)
+    reduce(0, open_values, lambda: own_values(0, 2, 8), more_values)
     h_one = x_ref[...].astype(jnp.float32) + total(0)
     h_scr[...] = h_one
     norm_into_lhs(h_one, g2_ref, b2_ref)
@@ -386,15 +419,15 @@
         slot = ring_wait(4 + chunk)
         for piece in range(4):
             acc[0] += jnp.dot(lhs[chunk * 4 + piece], ring[slot, piece], preferred_element_type=jnp.float32)
-        ring_start(4 + chunk + RING)
         return carry
     acc[0] = jnp.zeros_like(acc[0])
     lax.fori_loop(0, 4, query_step, 0)
+    for index in range(8, 8 + RING):
+        ring_start(jnp.int32(index))
     q_new = acc[0].astype(jnp.bfloat16)
     q_send[...] = q_new
     q_copy = pltpu.make_async_remote_copy(src_ref=q_send, dst_ref=q_recv, send_sem=ex_send.at[1], recv_sem=ex_recv.at[1], device_id=to_across, device_id_type=mesh_id)
     q_copy.start()
-    relay(1)
 
     def spread_query(side, q):
         wide = q.astype(jnp.float32)
@@ -402,23 +435,13 @@
             for span in range(spans):
                 q_scr[side, quad, span] = wide[span * 4:span * 4 + 4, quad * QUAD:(quad + 1) * QUAD]
     spread_query(0, q_new)
-    own_copies[1].wait()
-    own_values(1)
-    relay(2)
-    own_copies[2].wait()
-    own_copies[3].wait()
-    keys_and_scores(0, 0)
-    relay(3)
-    keys_and_scores(0, 1)
-    relay(4)
+    own_values(1, 2, 8)
     q_copy.wait()
     spread_query(1, q_recv[...])
-    keys_and_scores(1, dp)
-    relay(5)
-    for unit in range(4):
-        y_copy(unit).wait_recv()
-    keys_and_scores(1, other)
-    relay(6)
+    x_copy(0).wait()
+    y_copy(0).wait_recv()
+    keys_and_scores(1, 0)
+    keys_and_scores(1, 1)
 
     lane = lax.broadcasted_iota(jnp.int32, (128, 128), 1)
 
@@ -428,16 +451,17 @@
         part = jnp.sum(jnp.exp2((s - top) * rate), axis=-1, keepdims=True)
         return s, top, part
 
-    for side in range(2):
+    def st_copy(side):
+        return pltpu.make_async_remote_copy(src_ref=st_send.at[side], dst_ref=st_recv.at[side], send_sem=ex_send.at[2 * side], recv_sem=ex_recv.at[2 * side], device_id=to_across, device_id_type=mesh_id)
+
+    def send_stats(side):
         for quad in range(2):
             s, top, part = block_stats(side, quad)
             packed = jnp.where(lane == 0, top, jnp.where(lane == 1, part, 0.0))
             st_send[side, quad] = packed.T[0:8, :]
-    st_copy = pltpu.make_async_remote_copy(src_ref=st_send, dst_ref=st_recv, send_sem=ex_send.at[2], recv_sem=ex_recv.at[2], device_id=to_across, device_id_type=mesh_id)
-    st_copy.start()
-    relay(7)
-    st_copy.wait()
-    for side in range(2):
+        st_copy(side).start()
+
+    def weights_of(side):
         for quad in range(2):
             s, top, part = block_stats(side, quad)
             theirs = jnp.concatenate([st_recv[1 - side, quad], jnp.zeros((120, 128), jnp.float32)], axis=0).T
@@ -446,27 +470,37 @@
             whole = part * jnp.exp2((top - whole_top) * rate) + their_part * jnp.exp2((their_top - whole_top) * rate)
             p = jnp.exp2((s - whole_top) * rate) / whole
             p_scr[side, quad] = p.reshape(8, 16, 128)
+    send_stats(1)
+    own_copies[2].wait()
+    own_copies[3].wait()
+    keys_and_scores(0, 0)
+    keys_and_scores(0, 1)
+    send_stats(0)
+    st_copy(1).wait()
+    weights_of(0)
     apply_weights(0, 0, o_mine)
     apply_weights(0, 1, o_mine)
+    late_start()
+    st_copy(0).wait()
+    weights_of(1)
 
     def o_copy(slot, quad):
         return pltpu.make_async_remote_copy(src_ref=o_send.at[quad], dst_ref=o_recv.at[quad], send_sem=ex_send.at[3 + slot], recv_sem=ex_recv.at[3 + slot], device_id=to_across, device_id_type=mesh_id)
-    apply_weights(1, dp, o_send)
-    o_copy(0, dp).start()
-    for unit in range(4, 8):
-        y_copy(unit).wait_recv()
-    apply_weights(1, other, o_send)
-    o_copy(1, other).start()
-    o_copy(0, dp).wait()
-    o_copy(1, other).wait()
+    x_copy(1).wait()
+    y_copy(1).wait_recv()
+    apply_weights(1, 0, o_send)
+    o_copy(0, 0).start()
+    apply_weights(1, 1, o_send)
+    o_copy(1, 1).start()
+    o_copy(0, 0).wait()
+    o_copy(1, 1).wait()
     for quad in range(2):
         whole = o_mine[quad] + o_recv[quad]
         whole = jnp.concatenate([whole[span] for span in range(spans)], axis=0).astype(jnp.bfloat16)
         for piece in range(2):
             lhs[quad * 2 + piece] = whole[:, piece * CUT:(piece + 1) * CUT]
     stream_wide(8, 4)
-    reduce_open(1)
-    reduce_close(1)
+    reduce(1)
     h_two = h_scr[...] + total(1)
     h_scr[...] = h_two
     norm_into_lhs(h_two, g3_ref, b3_ref)
@@ -476,16 +510,15 @@
         u = (0.5 * u * (1.0 + lax.erf(u * (0.5 ** 0.5)))).astype(jnp.bfloat16)
         for chunk in range(4):
             lhs[piece * 4 + chunk] = u[:, chunk * CUT:(chunk + 1) * CUT]
-    stream_wide(28, 16)
-    reduce_open(2)
-    for unit in range(8):
-        x_copy(unit).wait_send()
-        y_copy(unit).wait_send()
-    reduce_close(2)
+    stream_wide(28, 16 - LATE)
+    late_finish()
+    reduce(2)
+    for kind in range(2):
+        y_copy(kind).wait_send()
     out_ref[...] = (h_scr[...] + total(2)).astype(jnp.bfloat16)
 
 
-def mix_block(x, self_out, nbr_enc, ln2_gain, ln2_bias, wq_c, wk_c, wv_c, w_o, wo_c, ln3_gain, ln3_bias, w_up, w_down):
+def mix_block(x, self_out, nbr_enc, enc_mate, wk_cross, wv_cross, ln2_gain, ln2_bias, wq_c, wk_c, wv_c, w_o, wo_c, ln3_gain, ln3_bias, w_up, w_down):
     batch, width = x.shape
     _, tokens, enc = nbr_enc.shape
     vmem = pl.BlockSpec(memory_space=pltpu.VMEM)
@@ -497,13 +530,12 @@
     return pl.pallas_call(
         mix_kernel,
         out_shape=jax.ShapeDtypeStruct((batch, width), bf),
-        in_specs=[vmem] * 6 + [hbm] * 8,
+        in_specs=[vmem] * 6 + [hbm] * 11,
         out_specs=vmem,
         scratch_shapes=[
-            pltpu.VMEM((RING, 4, CUT, SIDE), bf),
+            pltpu.VMEM((RING + LATE, 4, CUT, SIDE), bf),
             pltpu.VMEM((batch, 2 * tokens, enc), bf),
-            pltpu.VMEM((2, 2, 2, enc, QUAD), bf),
-            pltpu.VMEM((2, spans, 8 * tokens, QUAD), bf),
+            pltpu.VMEM((2, 2, enc, SIDE), bf),
             pltpu.VMEM((width // CUT, batch, CUT), bf),
             pltpu.VMEM((4, batch, SIDE), f32),
             pltpu.VMEM((batch, width), f32),
@@ -522,19 +554,21 @@
             pltpu.VMEM((3, batch, half), bf),
             pltpu.VMEM((3, batch, half), bf),
             pltpu.VMEM((3, 2, batch, half), bf),
-            dma((RING, 4)), dma, dma((2, 2)), dma((5,)), dma((5,)), dma((8,)), dma((8,)), dma((8,)), dma((8,)), dma((3, 3)), dma((3, 3)),
+            dma((RING + LATE, 4)), dma((2,)), dma((2, 2)), dma((2,)), dma((5,)), dma((5,)), dma((2,)), dma((2,)), dma((3, 3)), dma((3, 3)),
         ],
         compiler_params=pltpu.CompilerParams(vmem_limit_bytes=67043328, collective_id=0, has_side_effects=True),
         name='mix_block',
-    )(x, self_out, ln2_gain.reshape(1, width), ln2_bias.reshape(1, width), ln3_gain.reshape(1, width), ln3_bias.reshape(1, width), nbr_enc, w_o, wq_c, wk_c, wv_c, wo_c, w_up, w_down)
+    )(x, self_out, ln2_gain.reshape(1, width), ln2_bias.reshape(1, width), ln3_gain.reshape(1, width), ln3_bias.reshape(1, width), nbr_enc, enc_mate, wk_cross, wv_cross, w_o, wq_c, wk_c, wv_c, wo_c, w_up, w_down)
 
 
 def local_step(x, k_cache, v_cache, seq_lens, nbr_enc, ln1_gain, ln1_bias, w_q, w_k, w_v, w_o, ln2_gain, ln2_bias, wq_c, wk_c, wv_c, wo_c, ln3_gain, ln3_bias, w_up, w_down):
-    batch = x.shape[0]
-    heads, head_dim = k_cache.shape[2:]
+    rows = wk_c.shape[0] // 2
+    start = lax.axis_index('dp') * rows
+    wk_cross, wv_cross = [lax.ppermute(lax.dynamic_slice_in_dim(w, start, rows, 0), 'tp', [(0, 2), (1, 3), (2, 0), (3, 1)]) for w in (wk_c, wv_c)]
+    enc_mate = lax.ppermute(nbr_enc, 'tp', [(0, 1), (1, 0), (2, 3), (3, 2)])
     self_out, k_new, v_new = self_block(x, k_cache, v_cache, seq_lens, ln1_gain, ln1_bias, w_q, w_k, w_v)
-    layer_out = mix_block(x, self_out, nbr_enc, ln2_gain, ln2_bias, wq_c, wk_c, wv_c, w_o, wo_c, ln3_gain, ln3_bias, w_up, w_down)
-    return layer_out, k_new.reshape(batch, heads, head_dim), v_new.reshape(batch, heads, head_dim)
+    layer_out = mix_block(x, self_out, nbr_enc, enc_mate, wk_cross, wv_cross, ln2_gain, ln2_bias, wq_c, wk_c, wv_c, w_o, wo_c, ln3_gain, ln3_bias, w_up, w_down)
+    return layer_out, k_new, v_new
 
 
 def solution(mesh):

time: 179 us -> 149 us (0.83)
  Pallas kernels: 175 us -> 137 us
  waiting for transfers between devices: 0 us -> 4.08 us
  starting transfers between devices: 0 us -> 3.43 us
    pallas_call x1, Pallas kernels: 140 us -> 102 us  [mix_block(): pl.pallas_call(mix_kernel, out_shape=jax.ShapeDtypeStruct((batch, width),...]
    ppermute x0 -> x3, waiting for transfers between devices: none -> 4.08 us  [the longest x2 4.07 us: local_step(): lax.ppermute(lax.dynamic_slice_in_dim(w, start, rows, 0), 'tp', [(0, 2),...]
    ppermute x0 -> x3, starting transfers between devices: none -> 3.43 us  [the longest x2 3.4 us: local_step(): lax.ppermute(lax.dynamic_slice_in_dim(w, start, rows, 0), 'tp', [(0, 2),...]
    unnamed x3 -> x1, local copies, waits for them, and re-layouts: 4.63 us -> 1.67 us
    dynamic_slice x0 -> x2, local copies, waits for them, and re-layouts: none -> 2.48 us  [local_step(): lax.dynamic_slice_in_dim(w, start, rows, 0)]
  transfers between devices with their start and end apart: 0 -> 3, of which waited for: 0 -> 1; matrix products, arithmetic and copies ran while one was open for 0% -> 1% of each run, Pallas kernels for 0% -> 23%
where the time goes in v2:
time: 149 us
  Pallas kernels  137 us (92%)
  local copies, waits for them, and re-layouts  4.15 us (3%)
  waiting for transfers between devices  4.08 us (3%)
  starting transfers between devices  3.43 us (2%)
    pallas_call x1, Pallas kernels, mix_block(): pl.pallas_call(mix_kernel, out_shape=jax.ShapeDtypeStruct((batch, width),...  102 us
    pallas_call x1, Pallas kernels, self_block(): pl.pallas_call(attn_kernel, out_shape=(flat, new, new), in_specs=[pl.Bloc...  34.6 us
    ppermute x2, waiting for transfers between devices, local_step(): lax.ppermute(lax.dynamic_slice_in_dim(w, start, rows, 0), 'tp', [(0, 2),...  4.07 us
    ppermute x2, starting transfers between devices, local_step(): lax.ppermute(lax.dynamic_slice_in_dim(w, start, rows, 0), 'tp', [(0, 2),...  3.4 us
  transfers between devices with their start and end apart: 3, of which 1 were waited for; matrix products, arithmetic and copies ran while one was open for 1% of the time, Pallas kernels for 23%

profile of v2, /device:TPU:0, one launch (start us, length us, event | category | flops | bytes accessed | tf_op | source)
XLA Modules:
  0.0 149.1 jit_solution(2138571593868592665)
XLA Ops:
  0.6 1.2 constant_dynamic-slice_fusion
  1.9 3.4 %collective-permute-start.2 = (bf16[448,1024]{1,0:T(8,128)(2,1)S(1)}, bf16[448,1024]{1,0:T(8,128)(2,1)}, u32[]{:S(2)}, u32[]{:S(2)}) collective-permute-start(bf16[448,1024]{1,0:T(8,128)(2,1)S(1)} %constant_dynamic-slice_fusion), channel_id=1, source_target_pairs={{0,2},{1,3},{2,0},{3,1},{4,6},{5,7},{6,4},{7,5}} | collective-permute-start | bytes 2752520 | tf_op jit(solution)/shard_map/ppermute | solution.py:567
  5.2 1.2 constant_dynamic-slice_fusion.1
  6.5 0.0 collective-permute-start.1
  6.5 0.0 collective-permute-start
  6.6 34.6 %self_block.1 = (bf16[32,1024]{1,0:T(8,128)(2,1)}, bf16[32,8,128]{2,1,0:T(8,128)(2,1)}, bf16[32,8,128]{2,1,0:T(8,128)(2,1)}) custom-call(s32[32]{0:T(128)} %lens_ref.1, bf16[32,4096]{1,0:T(8,128)(2,1)} %x_ref.3, f32[1,4096]{1,0:T(1,128)} %bitcast.12, f32[1,4096]{1,0:T(1,128)} %bitcast.13, bf16[4096,1024]{1,0:T(8,128)(2,1)} %wq_ref.2, ...), custom_call_target="tpu_custom_call" | custom-call | flops 99999997952 | bytes 100000000 | tf_op jit(solution)/shard_map/self_block/pallas_call | solution.py:177
  41.2 0.0 collective-permute-done.2.wvx_ref
  41.2 4.1 %collective-permute-done.1.wkx_ref = bf16[448,1024]{1,0:T(8,128)(2,1)} collective-permute-done((bf16[448,1024]{1,0:T(8,128)(2,1)S(1)}, bf16[448,1024]{1,0:T(8,128)(2,1)}, u32[]{:S(2)}, u32[]{:S(2)}) %collective-permute-start.1) | collective-permute-done | bytes 917536 | tf_op jit(solution)/shard_map/ppermute | solution.py:567
  45.3 0.0 collective-permute-done.encm_ref
  45.3 102.1 %mix_block.1 = bf16[32,4096]{1,0:T(8,128)(2,1)} custom-call(bf16[32,4096]{1,0:T(8,128)(2,1)} %x_ref.3, bf16[32,1024]{1,0:T(8,128)(2,1)} %get-tuple-element.6.o_ref, f32[1,4096]{1,0:T(1,128)} %bitcast.8, f32[1,4096]{1,0:T(1,128)} %bitcast.9, f32[1,4096]{1,0:T(1,128)} %bitcast.10, f32[1,4096]{1,0:T(1,128)} %bitcast.11, bf16[32,64,896]{2,1,0:T(8,128)(2,1)} %enc_ref.1, ...), custom_call_target="tpu_custom_call" | custom-call | tf_op jit(solution)/shard_map/mix_block/pallas_call | solution.py:530
  147.4 1.7 %copy.25 = bf16[32,4096]{1,0:T(8,128)(2,1)} copy(bf16[32,4096]{1,0:T(8,128)(2,1)} %mix_block.1) | data formatting | bytes 524288
Async XLA Ops:
  1.9 39.3 %collective-permute-start.2 = (bf16[448,1024]{1,0:T(8,128)(2,1)S(1)}, bf16[448,1024]{1,0:T(8,128)(2,1)}, u32[]{:S(2)}, u32[]{:S(2)}) collective-permute-start(bf16[448,1024]{1,0:T(8,128)(2,1)S(1)} %constant_dynamic-slice_fusion), channel_id=1, source_target_pairs={{0,2},{1,3},{2,0},{3,1},{4,6},{5,7},{6,4},{7,5}} | collective-permute-start | bytes 2752520 | tf_op jit(solution)/shard_map/ppermute | solution.py:567
  6.5 38.8 %collective-permute-start.1 = (bf16[448,1024]{1,0:T(8,128)(2,1)S(1)}, bf16[448,1024]{1,0:T(8,128)(2,1)}, u32[]{:S(2)}, u32[]{:S(2)}) collective-permute-start(bf16[448,1024]{1,0:T(8,128)(2,1)S(1)} %constant_dynamic-slice_fusion.1), channel_id=1, source_target_pairs={{0,2},{1,3},{2,0},{3,1},{4,6},{5,7},{6,4},{7,5}} | collective-permute-start | bytes 2752520 | tf_op jit(solution)/shard_map/ppermute | solution.py:567
  6.5 38.7 %collective-permute-start = (bf16[32,64,896]{2,1,0:T(8,128)(2,1)}, bf16[32,64,896]{2,1,0:T(8,128)(2,1)}, u32[]{:S(2)}, u32[]{:S(2)}) collective-permute-start(bf16[32,64,896]{2,1,0:T(8,128)(2,1)} %enc_ref.1), channel_id=1, source_target_pairs={{0,1},{1,0},{2,3},{3,2},{4,5},{5,4},{6,7},{7,6}} | collective-permute-start | bytes 11010056 | tf_op jit(solution)/shard_map/ppermute | solution.py:568

commit v3 on v2

--- a/solution.py
+++ b/solution.py
@@ -207,11 +207,11 @@
 SIDE = 1024
 
 
-def mix_kernel(x_ref, o_ref, g2_ref, b2_ref, g3_ref, b3_ref, enc_ref, encm_ref, wkx_ref, wvx_ref, wo_ref, wq_ref, wk_ref, wv_ref, woc_ref, wup_ref, wdn_ref,
+def mix_kernel(x_ref, o_ref, g2_ref, b2_ref, g3_ref, b3_ref, enc_ref, encm_ref, wkx_ref, wo_ref, wq_ref, wk_ref, wv_ref, woc_ref, wup_ref, wdn_ref,
                out_ref,
                ring, e_buf, w_all, lhs, acc, h_scr, q_scr, q_send, q_recv, d_scr, p_scr, st_send, st_recv, o_mine, o_send, o_recv,
                ar_part, ar_half, ar_r1, ar_r2, ar_tot,
-               ring_sem, e_sem, w_sem, x_sem, ex_send, ex_recv, y_send, y_recv, ar_send, ar_recv):
+               ring_sem, e_sem, w_sem, x_sem, ex_send, ex_recv, y_send, y_recv, vx_send, vx_recv, vy_send, vy_recv, ar_send, ar_recv):
     batch, width = x_ref.shape
     head_dim = 128
     rate = head_dim ** -0.5 * LOG2_E
@@ -298,17 +298,28 @@
             own_copies.append(copy)
     pl.semaphore_wait(barrier, 3)
     half_rows = wkx_ref.shape[0]
-    crossed = (wkx_ref, wvx_ref)
+    unit_rows = half_rows // 4
     here = pl.ds(pl.multiple_of(dp * half_rows, half_rows), half_rows)
-
-    def x_copy(kind):
-        return pltpu.make_async_copy(crossed[kind], w_all.at[kind, 1, here, :], x_sem.at[kind])
-
-    def y_copy(kind):
-        return pltpu.make_async_remote_copy(src_ref=crossed[kind], dst_ref=w_all.at[kind, 1, here, :], send_sem=y_send.at[kind], recv_sem=y_recv.at[kind], device_id=to_other, device_id_type=mesh_id)
-
-    for kind in range(2):
-        y_copy(kind).start()
+    k_local = pltpu.make_async_copy(wkx_ref, w_all.at[0, 1, here, :], x_sem)
+    k_across = pltpu.make_async_remote_copy(src_ref=wkx_ref, dst_ref=w_all.at[0, 1, here, :], send_sem=y_send, recv_sem=y_recv, device_id=to_other, device_id_type=mesh_id)
+
+    def unit_place(unit):
+        return pl.ds(pl.multiple_of(dp * half_rows + unit * unit_rows, unit_rows), unit_rows)
+
+    def x_copy(unit):
+        rows = unit_place(unit)
+        return pltpu.make_async_remote_copy(src_ref=wv_ref.at[rows, :], dst_ref=w_all.at[1, 1, rows, :], send_sem=vx_send.at[unit], recv_sem=vx_recv.at[unit], device_id=to_across, device_id_type=mesh_id)
+
+    def y_copy(unit):
+        view = w_all.at[1, 1, unit_place(unit), :]
+        return pltpu.make_async_remote_copy(src_ref=view, dst_ref=view, send_sem=vy_send.at[unit], recv_sem=vy_recv.at[unit], device_id=to_other, device_id_type=mesh_id)
+
+    def relay(unit):
+        x_copy(unit).wait_recv()
+        y_copy(unit).start()
+
+    k_across.start()
+    x_copy(0).start()
 
     def ar_copy(which, stage):
         if stage == 0:
@@ -398,8 +409,7 @@
         ring_start(jnp.int32(index))
     for copy in own_copies[2:]:
         copy.start()
-    for kind in range(2):
-        x_copy(kind).start()
+    k_local.start()
 
     def open_values():
         e_local.wait()
@@ -411,6 +421,8 @@
         own_copies[1].wait()
         own_values(1, 0, 2)
     reduce(0, open_values, lambda: own_values(0, 2, 8), more_values)
+    x_copy(1).start()
+    relay(0)
     h_one = x_ref[...].astype(jnp.float32) + total(0)
     h_scr[...] = h_one
     norm_into_lhs(h_one, g2_ref, b2_ref)
@@ -428,6 +440,8 @@
     q_send[...] = q_new
     q_copy = pltpu.make_async_remote_copy(src_ref=q_send, dst_ref=q_recv, send_sem=ex_send.at[1], recv_sem=ex_recv.at[1], device_id=to_across, device_id_type=mesh_id)
     q_copy.start()
+    for unit in range(2, 4):
+        x_copy(unit).start()
 
     def spread_query(side, q):
         wide = q.astype(jnp.float32)
@@ -438,10 +452,13 @@
     own_values(1, 2, 8)
     q_copy.wait()
     spread_query(1, q_recv[...])
-    x_copy(0).wait()
-    y_copy(0).wait_recv()
+    relay(1)
+    k_local.wait()
+    k_across.wait_recv()
     keys_and_scores(1, 0)
+    relay(2)
     keys_and_scores(1, 1)
+    relay(3)
 
     lane = lax.broadcasted_iota(jnp.int32, (128, 128), 1)
 
@@ -486,8 +503,8 @@
 
     def o_copy(slot, quad):
         return pltpu.make_async_remote_copy(src_ref=o_send.at[quad], dst_ref=o_recv.at[quad], send_sem=ex_send.at[3 + slot], recv_sem=ex_recv.at[3 + slot], device_id=to_across, device_id_type=mesh_id)
-    x_copy(1).wait()
-    y_copy(1).wait_recv()
+    for unit in range(4):
+        y_copy(unit).wait_recv()
     apply_weights(1, 0, o_send)
     o_copy(0, 0).start()
     apply_weights(1, 1, o_send)
@@ -513,12 +530,14 @@
     stream_wide(28, 16 - LATE)
     late_finish()
     reduce(2)
-    for kind in range(2):
-        y_copy(kind).wait_send()
+    k_across.wait_send()
+    for unit in range(4):
+        x_copy(unit).wait_send()
+        y_copy(unit).wait_send()
     out_ref[...] = (h_scr[...] + total(2)).astype(jnp.bfloat16)
 
 
-def mix_block(x, self_out, nbr_enc, enc_mate, wk_cross, wv_cross, ln2_gain, ln2_bias, wq_c, wk_c, wv_c, w_o, wo_c, ln3_gain, ln3_bias, w_up, w_down):
+def mix_block(x, self_out, nbr_enc, enc_mate, wk_cross, ln2_gain, ln2_bias, wq_c, wk_c, wv_c, w_o, wo_c, ln3_gain, ln3_bias, w_up, w_down):
     batch, width = x.shape
     _, tokens, enc = nbr_enc.shape
     vmem = pl.BlockSpec(memory_space=pltpu.VMEM)
@@ -530,7 +549,7 @@
     return pl.pallas_call(
         mix_kernel,
         out_shape=jax.ShapeDtypeStruct((batch, width), bf),
-        in_specs=[vmem] * 6 + [hbm] * 11,
+        in_specs=[vmem] * 6 + [hbm] * 10,
         out_specs=vmem,
         scratch_shapes=[
             pltpu.VMEM((RING + LATE, 4, CUT, SIDE), bf),
@@ -554,20 +573,20 @@
             pltpu.VMEM((3, batch, half), bf),
             pltpu.VMEM((3, batch, half), bf),
             pltpu.VMEM((3, 2, batch, half), bf),
-            dma((RING + LATE, 4)), dma((2,)), dma((2, 2)), dma((2,)), dma((5,)), dma((5,)), dma((2,)), dma((2,)), dma((3, 3)), dma((3, 3)),
+            dma((RING + LATE, 4)), dma((2,)), dma((2, 2)), dma, dma((5,)), dma((5,)), dma, dma, dma((4,)), dma((4,)), dma((4,)), dma((4,)), dma((3, 3)), dma((3, 3)),
         ],
         compiler_params=pltpu.CompilerParams(vmem_limit_bytes=67043328, collective_id=0, has_side_effects=True),
         name='mix_block',
-    )(x, self_out, ln2_gain.reshape(1, width), ln2_bias.reshape(1, width), ln3_gain.reshape(1, width), ln3_bias.reshape(1, width), nbr_enc, enc_mate, wk_cross, wv_cross, w_o, wq_c, wk_c, wv_c, wo_c, w_up, w_down)
+    )(x, self_out, ln2_gain.reshape(1, width), ln2_bias.reshape(1, width), ln3_gain.reshape(1, width), ln3_bias.reshape(1, width), nbr_enc, enc_mate, wk_cross, w_o, wq_c, wk_c, wv_c, wo_c, w_up, w_down)
 
 
 def local_step(x, k_cache, v_cache, seq_lens, nbr_enc, ln1_gain, ln1_bias, w_q, w_k, w_v, w_o, ln2_gain, ln2_bias, wq_c, wk_c, wv_c, wo_c, ln3_gain, ln3_bias, w_up, w_down):
     rows = wk_c.shape[0] // 2
     start = lax.axis_index('dp') * rows
-    wk_cross, wv_cross = [lax.ppermute(lax.dynamic_slice_in_dim(w, start, rows, 0), 'tp', [(0, 2), (1, 3), (2, 0), (3, 1)]) for w in (wk_c, wv_c)]
+    wk_cross = lax.ppermute(lax.dynamic_slice_in_dim(wk_c, start, rows, 0), 'tp', [(0, 2), (1, 3), (2, 0), (3, 1)])
     enc_mate = lax.ppermute(nbr_enc, 'tp', [(0, 1), (1, 0), (2, 3), (3, 2)])
     self_out, k_new, v_new = self_block(x, k_cache, v_cache, seq_lens, ln1_gain, ln1_bias, w_q, w_k, w_v)
-    layer_out = mix_block(x, self_out, nbr_enc, enc_mate, wk_cross, wv_cross, ln2_gain, ln2_bias, wq_c, wk_c, wv_c, w_o, wo_c, ln3_gain, ln3_bias, w_up, w_down)
+    layer_out = mix_block(x, self_out, nbr_enc, enc_mate, wk_cross, ln2_gain, ln2_bias, wq_c, wk_c, wv_c, w_o, wo_c, ln3_gain, ln3_bias, w_up, w_down)
     return layer_out, k_new, v_new
 
 

time: 149 us -> 141 us (0.946); the launches traced: 149 us -> 143 us
  waiting for transfers between devices: 4.08 us -> 0.01 us
    pallas_call x1, Pallas kernels: 34.6 us -> 27.8 us  [self_block(): pl.pallas_call(attn_kernel, out_shape=(flat, new, new), in_specs=[pl.Bloc...]
    pallas_call x1, Pallas kernels: 102 us -> 108 us  [mix_block(): pl.pallas_call(mix_kernel, out_shape=jax.ShapeDtypeStruct((batch, width),...]
    ppermute x2 -> x1, waiting for transfers between devices: 4.07 us -> 0.01 us  [local_step(): lax.ppermute(lax.dynamic_slice_in_dim(wk_c, start, rows, 0), 'tp', [(0, 2...]
    ppermute x2 -> x1, starting transfers between devices: 3.4 us -> 3.36 us  [local_step(): lax.ppermute(lax.dynamic_slice_in_dim(wk_c, start, rows, 0), 'tp', [(0, 2...]
  transfers between devices with their start and end apart: 3 -> 2, of which waited for: 1 -> 0; matrix products, arithmetic and copies ran while one was open for 1% -> 0% of each run, Pallas kernels for 23% -> 19%
where the time goes in v3:
time: 141 us; the launch traced here: 143 us
  Pallas kernels  136 us (96%)
  starting transfers between devices  3.36 us (2%)
  local copies, waits for them, and re-layouts  2.91 us (2%)
    pallas_call x1, Pallas kernels, mix_block(): pl.pallas_call(mix_kernel, out_shape=jax.ShapeDtypeStruct((batch, width),...  108 us
    pallas_call x1, Pallas kernels, self_block(): pl.pallas_call(attn_kernel, out_shape=(flat, new, new), in_specs=[pl.Bloc...  27.8 us
    ppermute x1, starting transfers between devices, local_step(): lax.ppermute(lax.dynamic_slice_in_dim(wk_c, start, rows, 0), 'tp', [(0, 2...  3.36 us
  transfers between devices with their start and end apart: 2, of which 0 were waited for; matrix products, arithmetic and copies ran while one was open for 0% of the time, Pallas kernels for 19%

profile of v3, /device:TPU:0, one launch (start us, length us, event | category | flops | bytes accessed | tf_op | source)
XLA Modules:
  0.0 142.9 jit_solution(10612872808315263705)
XLA Ops:
  0.6 1.2 constant_dynamic-slice_fusion
  1.9 3.4 %collective-permute-start.1 = (bf16[448,1024]{1,0:T(8,128)(2,1)S(1)}, bf16[448,1024]{1,0:T(8,128)(2,1)}, u32[]{:S(2)}, u32[]{:S(2)}) collective-permute-start(bf16[448,1024]{1,0:T(8,128)(2,1)S(1)} %constant_dynamic-slice_fusion), channel_id=1, source_target_pairs={{0,2},{1,3},{2,0},{3,1},{4,6},{5,7},{6,4},{7,5}} | collective-permute-start | bytes 2752520 | tf_op jit(solution)/shard_map/ppermute | solution.py:586
  5.2 0.0 collective-permute-start
  5.2 27.8 %self_block.1 = (bf16[32,1024]{1,0:T(8,128)(2,1)}, bf16[32,8,128]{2,1,0:T(8,128)(2,1)}, bf16[32,8,128]{2,1,0:T(8,128)(2,1)}) custom-call(s32[32]{0:T(128)} %lens_ref.1, bf16[32,4096]{1,0:T(8,128)(2,1)} %x_ref.3, f32[1,4096]{1,0:T(1,128)} %bitcast.12, f32[1,4096]{1,0:T(1,128)} %bitcast.13, bf16[4096,1024]{1,0:T(8,128)(2,1)} %wq_ref.2, ...), custom_call_target="tpu_custom_call" | custom-call | flops 99999997952 | bytes 100000000 | tf_op jit(solution)/shard_map/self_block/pallas_call | solution.py:177
  33.0 0.0 collective-permute-done.1.wkx_ref
  33.0 0.0 collective-permute-done.encm_ref
  33.0 108.2 %mix_block.1 = bf16[32,4096]{1,0:T(8,128)(2,1)} custom-call(bf16[32,4096]{1,0:T(8,128)(2,1)} %x_ref.3, bf16[32,1024]{1,0:T(8,128)(2,1)} %get-tuple-element.6.o_ref, f32[1,4096]{1,0:T(1,128)} %bitcast.8, f32[1,4096]{1,0:T(1,128)} %bitcast.9, f32[1,4096]{1,0:T(1,128)} %bitcast.10, f32[1,4096]{1,0:T(1,128)} %bitcast.11, bf16[32,64,896]{2,1,0:T(8,128)(2,1)} %enc_ref.1, ...), custom_call_target="tpu_custom_call" | custom-call | tf_op jit(solution)/shard_map/mix_block/pallas_call | solution.py:549
  141.2 1.7 %copy.25 = bf16[32,4096]{1,0:T(8,128)(2,1)} copy(bf16[32,4096]{1,0:T(8,128)(2,1)} %mix_block.1) | data formatting | bytes 524288
Async XLA Ops:
  1.9 31.1 %collective-permute-start.1 = (bf16[448,1024]{1,0:T(8,128)(2,1)S(1)}, bf16[448,1024]{1,0:T(8,128)(2,1)}, u32[]{:S(2)}, u32[]{:S(2)}) collective-permute-start(bf16[448,1024]{1,0:T(8,128)(2,1)S(1)} %constant_dynamic-slice_fusion), channel_id=1, source_target_pairs={{0,2},{1,3},{2,0},{3,1},{4,6},{5,7},{6,4},{7,5}} | collective-permute-start | bytes 2752520 | tf_op jit(solution)/shard_map/ppermute | solution.py:586
  5.2 27.8 %collective-permute-start = (bf16[32,64,896]{2,1,0:T(8,128)(2,1)}, bf16[32,64,896]{2,1,0:T(8,128)(2,1)}, u32[]{:S(2)}, u32[]{:S(2)}) collective-permute-start(bf16[32,64,896]{2,1,0:T(8,128)(2,1)} %enc_ref.1), channel_id=1, source_target_pairs={{0,1},{1,0},{2,3},{3,2},{4,5},{5,4},{6,7},{7,6}} | collective-permute-start | bytes 11010056 | tf_op jit(solution)/shard_map/ppermute | solution.py:587
